TPU v7x, 128 devices: a whole 4x4x4 slice. The times are simulated.
128 devices in a mesh: samp: 4 (over z), row: 4 (over x_lo, core), col: 8 (over x_hi, y).
Axes of the slice: x: 4 (x_hi: 2, x_lo: 2; x = x_hi * 2 + x_lo), y: 4, z: 4, core: 2. Of those that a mesh axis runs over, the one named last changes fastest.
Arguments:
- pair: float32 [4, 320, 320, 128], P('samp', 'row', 'col'), may hold values from -6 to 6
- cotangent: float32 [4, 320, 320, 128], P('samp', 'row', 'col'), may hold values from -6 to 6
- crop_length: int32 [4], P('samp'), may hold values from 160 to 320
- in_gain: float32 [128], replicated, may hold values from 0.5 to 1.5
- in_bias: float32 [128], replicated, may hold values from -1.5 to 1.5
- proj_weight: bfloat16 [128, 512], replicated, may hold values from -0.5 to 0.5
- gate_weight: bfloat16 [128, 128], replicated, may hold values from -0.5 to 0.5
- out_gain: float32 [128], replicated, may hold values from 0.5 to 1.5
- out_bias: float32 [128], replicated, may hold values from -1.5 to 1.5
- out_weight: bfloat16 [128, 128], replicated, may hold values from -0.5 to 0.5
Outputs:
- grad_pair: float32 [4, 320, 320, 128], P('samp', 'row', 'col')
- grad_in_gain: float32 [128], replicated
- grad_in_bias: float32 [128], replicated
- grad_proj_weight: float32 [128, 512], replicated
- grad_gate_weight: float32 [128, 128], replicated
- grad_out_gain: float32 [128], replicated
- grad_out_bias: float32 [128], replicated
- grad_out_weight: float32 [128, 128], replicated
All inputs are finite; a program needn't handle non-finite values.
Results may differ from a plain program's by a relative error of at most 0.012.
Values may be sent and summed in bfloat16 or wider, within the bound.
No kernel may reach another device: no remote copies, remote signals or barrier semaphores. Data moves between devices by JAX's collectives and lax.ppermute only.
A program may use at most 128 MiB of HBM per device.

v0:
```python
import jax
import jax.numpy as jnp
from jax import lax
from jax.sharding import PartitionSpec as P

epsilon = 1e-05


def cut_along(shard, dim, length):
    before, after = (shard.shape[:dim], shard.shape[dim + 1 :])
    return jnp.moveaxis(shard.reshape(*before, length, -1, *after), dim, 0)


def piece_ends(length, count):
    unit = 8 if length >= 8 * count else 1
    return [length // unit * k // count * unit for k in range(1, count)]


def joined_along(parts, dim):
    parts = jnp.moveaxis(parts, 0, dim)
    lengths = parts.shape
    return parts.reshape(*lengths[:dim], lengths[dim] * lengths[dim + 1], *lengths[dim + 2 :])


def cut_exchange(shard, axis, pieces, split_dim, concat_dim):
    parts = cut_along(shard, split_dim, lax.axis_size(axis))
    widest = max(range(1, max(2, parts.ndim - 1)), key=lambda d: parts.shape[d])
    finished = []
    for share in jnp.split(parts, piece_ends(parts.shape[widest], pieces), axis=widest):
        if share.size:
            finished.append(lax.all_to_all(share, axis, split_axis=0, concat_axis=0, tiled=True))
    return joined_along(jnp.concatenate(finished, axis=widest), concat_dim)


def packed_total(arrays, axis):
    line, at, finished = (jnp.concatenate([a.reshape(-1) for a in arrays]), 0, [])
    subtotal = lax.psum(line, axis)
    for a in arrays:
        finished.append(subtotal[at : at + a.size].reshape(a.shape))
        at += a.size
    return tuple(finished)


def norm_stats(values):
    centre = jnp.mean(values, axis=-1, keepdims=True)
    centered = values - centre
    variance = jnp.mean(centered * centered, axis=-1, keepdims=True)
    inverse = lax.rsqrt(variance + epsilon)
    return (centered * inverse, inverse)


def norm_back(upstream, normal, inverse, weights):
    scaled = upstream * weights
    return inverse * (
        scaled
        - jnp.mean(scaled, axis=-1, keepdims=True)
        - normal * jnp.mean(scaled * normal, axis=-1, keepdims=True)
    )


def per_device(
    pair,
    cotangent,
    crop_length,
    in_gain,
    in_bias,
    proj_weight,
    gate_weight,
    out_gain,
    out_bias,
    out_weight,
):
    pair_tile = pair[0]
    upstream = cotangent[0]
    height, breadth, channels = pair_tile.shape
    hidden = out_weight.shape[0]
    row_first = lax.axis_index("row") * height
    col_first = lax.axis_index("col") * breadth
    crop_end = crop_length[0]
    row_live = (row_first + jnp.arange(height, dtype=jnp.int32) < crop_end).astype(jnp.float32)
    col_live = (col_first + jnp.arange(breadth, dtype=jnp.int32) < crop_end).astype(jnp.float32)
    live_mask = row_live[:, None, None] * col_live[None, :, None]
    in_hat, in_scale = norm_stats(pair_tile)
    normed = (in_hat * in_gain + in_bias).astype(jnp.bfloat16)
    flat_normed = normed.reshape(-1, channels)
    projected = jnp.dot(flat_normed, proj_weight, preferred_element_type=jnp.float32).reshape(
        height, breadth, 4 * hidden
    )
    left_sig = jax.nn.sigmoid(projected[..., :hidden])
    left_value = projected[..., hidden : 2 * hidden]
    right_sig = jax.nn.sigmoid(projected[..., 2 * hidden : 3 * hidden])
    right_value = projected[..., 3 * hidden :]
    left_factor = (left_sig * left_value * live_mask).astype(jnp.bfloat16)
    right_factor = (right_sig * right_value * live_mask).astype(jnp.bfloat16)
    right_rows = lax.all_gather(right_factor, "row", axis=0, tiled=True)
    right_turned = cut_exchange(right_rows, "col", 2, 0, 1)
    left_rows = lax.all_gather(left_factor, "col", axis=1, tiled=True)
    product = jnp.einsum(
        "ikh,jkh->ijh", left_rows, right_turned, preferred_element_type=jnp.float32
    )
    tri_hat, tri_scale = norm_stats(product)
    tri_normed = (tri_hat * out_gain + out_bias).astype(jnp.bfloat16)
    flat_tri = tri_normed.reshape(-1, hidden)
    out_value = jnp.dot(flat_tri, out_weight, preferred_element_type=jnp.float32)
    gate_value = jax.nn.sigmoid(
        jnp.dot(flat_normed, gate_weight, preferred_element_type=jnp.float32)
    )
    flat_up = upstream.reshape(-1, channels)
    d_out = (flat_up * gate_value).astype(jnp.bfloat16)
    d_gate = (flat_up * out_value * gate_value * (1.0 - gate_value)).astype(jnp.bfloat16)
    g_out_weight = jnp.dot(flat_tri.T, d_out, preferred_element_type=jnp.float32)
    d_tri_normed = jnp.dot(d_out, out_weight.T, preferred_element_type=jnp.float32).reshape(
        height, breadth, hidden
    )
    g_out_gain = jnp.sum(d_tri_normed * tri_hat, axis=(0, 1))
    g_out_bias = jnp.sum(d_tri_normed, axis=(0, 1))
    d_product = norm_back(d_tri_normed, tri_hat, tri_scale, out_gain).astype(jnp.bfloat16)
    grad_full = lax.all_gather(d_product, "col", axis=1, tiled=True)
    d_left = jnp.einsum("ijh,jkh->ikh", grad_full, right_rows, preferred_element_type=jnp.float32)
    d_right = lax.psum_scatter(
        jnp.einsum(
            "ijh,ikh->jkh", grad_full, left_factor, preferred_element_type=jnp.float32
        ).astype(jnp.bfloat16),
        "row",
        scatter_dimension=0,
        tiled=True,
    ).astype(jnp.float32)
    d_proj = (
        jnp.concatenate(
            [
                d_left * live_mask * left_value * left_sig * (1.0 - left_sig),
                d_left * live_mask * left_sig,
                d_right * live_mask * right_value * right_sig * (1.0 - right_sig),
                d_right * live_mask * right_sig,
            ],
            axis=-1,
        )
        .astype(jnp.bfloat16)
        .reshape(-1, 4 * hidden)
    )
    g_proj_weight = jnp.dot(flat_normed.T, d_proj, preferred_element_type=jnp.float32)
    g_gate_weight = jnp.dot(flat_normed.T, d_gate, preferred_element_type=jnp.float32)
    d_normed = (
        jnp.dot(d_proj, proj_weight.T, preferred_element_type=jnp.float32)
        + jnp.dot(d_gate, gate_weight.T, preferred_element_type=jnp.float32)
    ).reshape(height, breadth, channels)
    g_in_gain = jnp.sum(d_normed * in_hat, axis=(0, 1))
    g_in_bias = jnp.sum(d_normed, axis=(0, 1))
    grad_pair = norm_back(d_normed, in_hat, in_scale, in_gain)
    totals = packed_total(
        (g_in_gain, g_in_bias, g_proj_weight, g_gate_weight, g_out_gain, g_out_bias, g_out_weight),
        ("samp", "row", "col"),
    )
    factor = 1.0 / (breadth * lax.axis_size("col"))
    return (
        grad_pair[None],
        totals[0] * factor,
        totals[1] * factor,
        totals[2] * factor,
        totals[3] * factor,
        totals[4] * factor,
        totals[5] * factor,
        totals[6] * factor,
    )


def solution(mesh):
    return jax.shard_map(
        per_device,
        mesh=mesh,
        in_specs=(
            P("samp", "row", "col", None),
            P("samp", "row", "col", None),
            P("samp"),
            P(),
            P(),
            P(),
            P(),
            P(),
            P(),
            P(),
        ),
        out_specs=(P("samp", "row", "col", None), P(), P(), P(), P(), P(), P(), P()),
        check_vma=False,
    )
```

profile of v0, /device:TPU:1, one launch (start us, length us, event | category | flops | bytes accessed | tf_op | source)
XLA Modules:
  0.0 551.7 jit_solution(769624488051377025)
XLA Ops:
  7.3 2.0 reduce_sum.108
  11.1 1.3 fusion.33
  12.4 2.5 multiply_convert_fusion.5
  16.4 42.1 %all-gather.4.cloned.1.call-done = bf16[320,40,128]{2,1,0:T(8,128)(2,1)} async-done(((bf16[80,40,128]{2,1,0:T(8,128)(2,1)}), bf16[320,40,128]{2,1,0:T(8,128)(2,1)}) %all-gather.4.cloned.1.call-update) | async-done | bytes 3276816 | tf_op jit(solution)/shard_map/all_gather | solution.py:95
  58.5 2.5 split.8
  61.0 6.1 %all-to-all-start = ((bf16[8,16,40,128]{3,2,1,0:T(8,128)(2,1)}), bf16[8,16,40,128]{3,2,1,0:T(8,128)(2,1)S(1)}, u32[]{:S(2)}, u32[]{:S(2)}) async-start(bf16[8,16,40,128]{3,2,1,0:T(8,128)(2,1)} %split.8), calls=%async_computation | async-start | bytes 2621440 | tf_op jit(solution)/shard_map/all_to_all | solution.py:31
  67.4 3.2 split.9
  70.6 23.4 %all-to-all-done = bf16[8,16,40,128]{3,2,1,0:T(8,128)(2,1)S(1)} async-done(((bf16[8,16,40,128]{3,2,1,0:T(8,128)(2,1)}), bf16[8,16,40,128]{3,2,1,0:T(8,128)(2,1)S(1)}, u32[]{:S(2)}, u32[]{:S(2)}) %all-to-all-start) | async-done | bytes 1310752 | tf_op jit(solution)/shard_map/all_to_all | solution.py:31
  94.0 4.3 all-to-all-start.1
  98.6 1.8 add_convert_fusion.1
  100.4 1.8 fusion.29
  103.1 1.1 fusion.39
  104.2 2.1 copy.73
  106.5 19.8 %all-to-all-done.1 = bf16[8,24,40,128]{3,2,1,0:T(8,128)(2,1)} async-done(((bf16[8,24,40,128]{3,2,1,0:T(8,128)(2,1)}), bf16[8,24,40,128]{3,2,1,0:T(8,128)(2,1)}, u32[]{:S(2)}, u32[]{:S(2)}) %all-to-all-start.1) | async-done | bytes 1966112 | tf_op jit(solution)/shard_map/all_to_all | solution.py:31
  126.3 1.8 pad_maximum_fusion
  129.1 4.4 copy.67
  133.5 38.1 %all-gather.6.cloned.1.call-done = bf16[80,320,128]{2,1,0:T(8,128)(2,1)} async-done(((bf16[80,40,128]{2,1,0:T(8,128)(2,1)}), bf16[80,320,128]{2,1,0:T(8,128)(2,1)}) %all-gather.6.cloned.1.call-update) | async-done | bytes 6553616 | tf_op jit(solution)/shard_map/all_gather | solution.py:97
  171.6 14.4 %copy.68 = bf16[80,320,128]{0,1,2:T(8,128)(2,1)} copy(bf16[80,320,128]{2,1,0:T(8,128)(2,1)} %all-gather.6.cloned.1.call-done) | data formatting | bytes 13107200 | tf_op jit(solution)/shard_map/all_gather | solution.py:97
  186.0 7.3 %bitcast_reduce_fusion = (f32[80,40]{0,1:T(8,128)S(1)}, f32[128,40,80]{2,1,0:T(8,128)S(1)}) fusion(bf16[40,320,128]{1,0,2:T(8,128)(2,1)} %copy.67, bf16[80,320,128]{0,1,2:T(8,128)(2,1)} %copy.68), kind=kOutput, calls=%fused_computation.27 | convolution fusion | flops 262550400 | bytes 11481600 | tf_op jit(solution)/shard_map/ikh,jkh->ijh/dot_general | solution.py:98
  194.1 3.6 multiply_reduce_fusion
  197.9 4.3 multiply_convert_fusion
  203.4 1.4 copy.79
  204.8 119.7 %all-gather.8.cloned.1.call-done = bf16[80,320,128]{0,1,2:T(8,128)(2,1)} async-done(((bf16[80,40,128]{0,1,2:T(8,128)(2,1)}), bf16[80,320,128]{0,1,2:T(8,128)(2,1)}) %all-gather.8.cloned.1.call-update) | async-done | bytes 6553616 | tf_op jit(solution)/shard_map/all_gather | solution.py:118
  324.5 9.2 %fusion.41 = bf16[128,40,320]{2,1,0:T(8,128)(2,1)} fusion(bf16[80,40,128]{0,1,2:T(8,128)(2,1)S(1)} %copy.79, bf16[80,320,128]{0,1,2:T(8,128)(2,1)} %all-gather.8.cloned.1.call-done), kind=kOutput, calls=%fused_computation.99 | convolution fusion | flops 262144000 | bytes 10649600 | tf_op jit(solution)/shard_map/ijh,ikh->jkh/dot_general | solution.py:121
  333.7 6.7 %copy.80 = bf16[128,40,320]{0,1,2:T(8,128)(2,1)} copy(bf16[128,40,320]{2,1,0:T(8,128)(2,1)} %fusion.41) | data formatting | bytes 6553600 | tf_op jit(solution)/shard_map/ijh,ikh->jkh/dot_general | solution.py:121
  340.4 1.8 copy-done.5
  342.3 4.9 copy.77
  347.2 2.8 copy.81
  350.0 1.0 convolution_bitcast_fusion
  351.1 1.9 fusion.5
  354.1 1.5 fusion.42
  355.7 5.4 fusion.40
  361.1 2.0 copy.78
  363.1 14.1 %reduce-scatter.2.cloned.1.call-done = bf16[80,40,128]{2,1,0:T(8,128)(2,1)} async-done(((bf16[320,40,128]{2,1,0:T(8,128)(2,1)}), bf16[80,40,128]{2,1,0:T(8,128)(2,1)}) %reduce-scatter.2.cloned.1.call-update) | async-done | bytes 819216 | tf_op jit(solution)/shard_map/reduce_scatter | solution.py:120
  377.2 4.4 multiply_convert_fusion.4
  381.7 1.6 fusion.30
  383.5 2.0 multiply_reduce_fusion.3
  385.4 1.3 constant_dynamic-update-slice_fusion.6
  386.7 1.3 constant_dynamic-update-slice_fusion.5
  388.0 1.7 constant_dynamic-update-slice_fusion.4
  389.7 1.5 constant_dynamic-update-slice_fusion.3
  391.3 1.3 constant_dynamic-update-slice_fusion.2
  392.6 1.3 constant_dynamic-update-slice_fusion.1
  393.9 1.5 constant_dynamic-update-slice_fusion
  397.5 4.1 subtract_multiply_fusion
  401.6 138.9 %all-reduce.2.cloned.1.call-done = f32[98816]{0:T(1024)} async-done(((f32[98816]{0:T(1024)}), f32[98816]{0:T(1024)}) %all-reduce.2.cloned.1.call-update) | async-done | bytes 395280 | tf_op jit(solution)/shard_map/psum | solution.py:37
  542.3 1.6 fusion.35
  543.9 1.3 slice_multiply_fusion.3
  (103 shorter events, 12.1 us)
Async XLA Ops:
  7.2 3.9 copy-start
  7.2 2.1 copy-start.2
  7.2 51.4 %all-gather.4.cloned.1.call-start = ((), (), s32[]{:S(2)}) async-start(), calls=%async_computation.3 | async-start | bytes 4096000 | tf_op jit(solution)/shard_map/all_gather | solution.py:95
  7.2 3.8 copy-start.25
  7.3 3.8 copy-start.27
  12.4 3.3 copy-start.1
  15.7 155.9 %all-gather.6.cloned.1.call-start = ((), (), s32[]{:S(2)}) async-start(), calls=%async_computation.4 | async-start | bytes 7372800 | tf_op jit(solution)/shard_map/all_gather | solution.py:97
  61.0 32.9 %all-to-all-start = ((bf16[8,16,40,128]{3,2,1,0:T(8,128)(2,1)}), bf16[8,16,40,128]{3,2,1,0:T(8,128)(2,1)S(1)}, u32[]{:S(2)}, u32[]{:S(2)}) async-start(bf16[8,16,40,128]{3,2,1,0:T(8,128)(2,1)} %split.8), calls=%async_computation | async-start | bytes 2621440 | tf_op jit(solution)/shard_map/all_to_all | solution.py:31
  67.3 31.3 %copy-start.18 = (f32[3200]{0:T(1024)}, f32[3200]{0:T(1024)S(1)}, u32[]{:S(2)}) copy-start(f32[3200]{0:T(1024)S(1)} %rsqrt.22) | copy-start | bytes 38404
  67.4 31.2 %copy-start.20 = (f32[3200]{0:T(1024)}, f32[3200]{0:T(1024)S(1)}, u32[]{:S(2)}) copy-start(f32[3200]{0:T(1024)S(1)} %div.47) | copy-start | bytes 38404
  94.0 32.4 %all-to-all-start.1 = ((bf16[8,24,40,128]{3,2,1,0:T(8,128)(2,1)}), bf16[8,24,40,128]{3,2,1,0:T(8,128)(2,1)}, u32[]{:S(2)}, u32[]{:S(2)}) async-start(bf16[8,24,40,128]{3,2,1,0:T(8,128)(2,1)} %split.9), calls=%async_computation.1 | async-start | bytes 3932160 | tf_op jit(solution)/shard_map/all_to_all | solution.py:31
  98.3 2.0 copy-start.22
  98.3 226.1 %all-gather.8.cloned.1.call-start = ((), (), s32[]{:S(2)}) async-start(), calls=%async_computation.5 | async-start | bytes 11796480 | tf_op jit(solution)/shard_map/all_gather | solution.py:118
  98.6 1.8 copy-start.11
  100.4 1.8 copy-start.7
  100.4 2.7 copy-start.16
  100.4 2.7 copy-start.24
  102.2 0.9 copy-start.9
  194.1 3.8 copy-start.29
  202.2 1.1 copy-start.6
  202.2 175.0 %reduce-scatter.2.cloned.1.call-start = ((), (), s32[]{:S(2)}) async-start(), calls=%async_computation.6 | async-start | bytes 4096000 | tf_op jit(solution)/shard_map/reduce_scatter | solution.py:120
  340.4 1.9 copy-start.5
  340.4 200.2 %all-reduce.2.cloned.1.call-start = ((), (), s32[]{:S(2)}) async-start(), calls=%async_computation.7 | async-start | bytes 794624 | tf_op jit(solution)/shard_map/psum | solution.py:37
  347.2 2.9 copy-start.10
  347.2 3.9 copy-start.12
  350.0 1.1 copy-start.17
  351.1 2.0 copy-start.8
  351.1 3.0 copy-start.23
  353.1 2.6 copy-start.4
  363.1 18.5 %copy-start.3 = (f32[1,80,40,128]{3,2,1,0:T(8,128)S(1)}, f32[1,80,40,128]{3,2,1,0:T(8,128)}, u32[]{:S(2)}) copy-start(f32[1,80,40,128]{3,2,1,0:T(8,128)} %param.10) | copy-start | bytes 4915204
  363.1 18.5 %copy-start.26 = (f32[128]{0:T(128)S(1)}, f32[128]{0:T(128)}, u32[]{:S(2)}) copy-start(f32[128]{0:T(128)} %param.13) | copy-start | bytes 1540
  363.1 18.5 %copy-start.28 = (f32[128]{0:T(128)S(1)}, f32[128]{0:T(128)}, u32[]{:S(2)}) copy-start(f32[128]{0:T(128)} %param.14) | copy-start | bytes 1540
  381.7 1.7 copy-start.13
  381.7 1.7 copy-start.19
  381.7 1.7 copy-start.21
  383.4 6.3 %copy-start.15 = (f32[16384]{0:T(1024)S(1)}, f32[16384]{0:T(1024)}, u32[]{:S(2)}) copy-start(f32[16384]{0:T(1024)} %convolution_bitcast_fusion.1) | copy-start | bytes 196612
  383.4 7.8 %copy-start.31 = (f32[128]{0:T(128)S(1)}, f32[128]{0:T(128)}, u32[]{:S(2)}) copy-start(f32[128]{0:T(128)} %get-tuple-element.8) | copy-start | bytes 1540
  383.5 9.1 %copy-start.30 = (f32[128]{0:T(128)S(1)}, f32[128]{0:T(128)}, u32[]{:S(2)}) copy-start(f32[128]{0:T(128)} %get-tuple-element.13) | copy-start | bytes 1540
  383.5 10.4 %copy-start.14 = (f32[16384]{0:T(1024)S(1)}, f32[16384]{0:T(1024)}, u32[]{:S(2)}) copy-start(f32[16384]{0:T(1024)} %convolution_bitcast_fusion) | copy-start | bytes 196612
Sparse Core Ops, SparseCore 0:
  15.8 42.7 all-gather.3
  61.0 110.5 all-gather.5
  202.4 122.0 all-gather.7
  340.5 36.6 reduce-scatter.1
  395.5 144.9 all-reduce.1
where the time goes:
time: 553 us; the launch traced here: 552 us
  waiting for transfers between devices  397 us (72%)
  local copies, waits for them, and re-layouts  62.9 us (11%)
  matrix products  35.3 us (6%)
  other arithmetic  30.6 us (6%)
  between operations  15 us (3%)
  starting transfers between devices  11.1 us (2%)
    psum x1, waiting for transfers between devices, packed_total(): subtotal = lax.psum(line, axis)  139 us
    all_gather x1, waiting for transfers between devices, per_device(): grad_full = lax.all_gather(d_product, 'col', axis=1, tiled=True)  120 us
    all_to_all x2, waiting for transfers between devices, cut_exchange(): lax.all_to_all(share, axis, split_axis=0, concat_axis=0, tiled=True)  43.2 us
    all_gather x1, waiting for transfers between devices, per_device(): right_rows = lax.all_gather(right_factor, 'row', axis=0, tiled=True)  42.1 us
    all_gather x1, waiting for transfers between devices, per_device(): left_rows = lax.all_gather(left_factor, 'col', axis=1, tiled=True)  38.1 us
    all_gather x1, local copies, waits for them, and re-layouts, per_device(): left_rows = lax.all_gather(left_factor, 'col', axis=1, tiled=True)  14.4 us
    reduce_scatter x1, waiting for transfers between devices, per_device(): lax.psum_scatter(jnp.einsum('ijh,ikh->jkh', grad_full, left_factor, prefe...  14.1 us
    unnamed x71, local copies, waits for them, and re-layouts  12.9 us
  transfers between devices with their start and end apart: 7, of which 7 were waited for; matrix products, arithmetic and copies ran while one was open for 9% of the time, Pallas kernels for 0%

commit v1 on v0

v1 whole, which is shorter than its diff:
```python
import functools

import jax
import jax.numpy as jnp
from jax import lax
from jax.experimental import pallas as pl
from jax.experimental.pallas import tpu as pltpu
from jax.sharding import PartitionSpec as P

epsilon = 1e-05

TALL = 80
WIDE = 40
CH = 128
ROWS = 4
COLS = 8
PEERS = ROWS * COLS
OWN = CH // PEERS
CELLS = TALL * WIDE
STEP = 8 * TALL
STEPS = CELLS // STEP
FULL = COLS * WIDE
PITCH = FULL + 8
JPITCH = ROWS * 128 + 8
f32 = jnp.float32
bf16 = jnp.bfloat16


def mm(a, b, ca, cb):
    return lax.dot_general(a, b, (((ca,), (cb,)), ((), ())), preferred_element_type=f32)


def sigmoid(x):
    return 0.5 * jnp.tanh(0.5 * x) + 0.5


def column(row):
    return jnp.broadcast_to(row, (CH, CH)).T


def wide(col):
    return jnp.concatenate([col] * (STEP // CH), axis=1)


def interleave():
    n = 2 * CH
    q = lax.broadcasted_iota(jnp.int32, (n, n), 0)
    p = lax.broadcasted_iota(jnp.int32, (n, n), 1)
    src = ((q >> 2) & 1) * CH + (q >> 3) * OWN + (q & 3)
    return jnp.where(src == p, 1.0, 0.0).astype(bf16)


def turned(ref):
    flat = ref.reshape(STEP, CH)
    rows = [flat[pl.ds(k, TALL, stride=8), :] for k in range(8)]
    return jnp.concatenate(rows, axis=0).T


def live_cells(lim_ref, g):
    lane = lax.broadcasted_iota(jnp.int32, (1, STEP), 1)
    k = jnp.zeros((1, STEP), jnp.int32)
    for m in range(1, 8):
        k = k + jnp.where(lane >= m * TALL, 1, 0)
    i = lane - k * TALL
    live = jnp.logical_and(i < lim_ref[0], k + g * 8 < lim_ref[1])
    return jnp.where(live, 1.0, 0.0).astype(f32)


def hat_of(x):
    centre = jnp.mean(x, axis=0, keepdims=True)
    centered = x - centre
    inverse = lax.rsqrt(jnp.mean(centered * centered, axis=0, keepdims=True) + epsilon)
    return centered * inverse, inverse


def lane_fold(x):
    out = x[:, :CH]
    for m in range(1, x.shape[1] // CH):
        out = out + x[:, m * CH : (m + 1) * CH]
    return out


def peers_of(s):
    return s >> 3, s & 7


def unfold(rows):
    n = rows.shape[0]
    lane = lax.broadcasted_iota(jnp.int32, (n, 128), 1)
    out = []
    for k in range(8):
        at = k * TALL
        m, off = at // 128, at % 128
        v = rows[:, m * 128 : (m + 1) * 128]
        if off + TALL > 128:
            v = jnp.where(lane >= off, v, rows[:, (m + 1) * 128 : (m + 2) * 128])
        out.append(pltpu.roll(v, 128 - off, 1) if off else v)
    return out


def fold(pieces):
    n = pieces[0].shape[0]
    lane = lax.broadcasted_iota(jnp.int32, (n, 128), 1)
    r = [pltpu.roll(p, (k * TALL) % 128, 1) if k else p for k, p in enumerate(pieces)]
    cols = []
    for m in range(STEP // 128):
        lo, hi = m * 128, (m + 1) * 128
        v = None
        for k in range(8):
            a, b = max(lo, k * TALL), min(hi, (k + 1) * TALL)
            if a >= b:
                continue
            v = r[k] if v is None else jnp.where(lane >= a - lo, r[k], v)
        cols.append(v)
    return jnp.concatenate(cols, axis=1)


def k1(lim_ref, pair_ref, cot_ref, ig_ref, ib_ref, w_ref, gw_ref, f_ref, do_ref, e_ref, wg_s, wv_s, gw_s, v_s):
    g = pl.program_id(0)

    @pl.when(g == 0)
    def _():
        perm = interleave()
        w = w_ref[...]
        gates = jnp.concatenate([w[:, :CH], w[:, 2 * CH : 3 * CH]], axis=1)
        values = jnp.concatenate([w[:, CH : 2 * CH], w[:, 3 * CH :]], axis=1)
        wg_s[...] = mm(perm, gates, 1, 1).astype(bf16)
        wv_s[...] = mm(perm, values, 1, 1).astype(bf16)
        gw_s[...] = gw_ref[...].astype(f32).T.astype(bf16)
        v_s[0] = column(ig_ref[...])
        v_s[1] = column(ib_ref[...])

    hat, _ = hat_of(turned(pair_ref))
    normed = (hat * wide(v_s[0]) + wide(v_s[1])).astype(bf16)
    live = live_cells(lim_ref, g)
    value = mm(wv_s[...], normed, 1, 0) * live
    factor = sigmoid(mm(wg_s[...], normed, 1, 0)) * value
    f_ref[...] = factor.astype(bf16).reshape(PEERS, 2 * OWN, STEP)
    gate = sigmoid(mm(gw_s[...], normed, 1, 0))
    up = turned(cot_ref) * gate
    do_ref[...] = up.astype(bf16)
    e_ref[...] = up * (1.0 - gate)


def k2(y_ref, l_ref, r_ref, z_ref, x_s, p_s):
    def spread(s, carry):
        r, c = peers_of(s)
        rows = y_ref[s].astype(f32)
        for g in range(STEPS):
            for k, v in enumerate(unfold(rows[:, g * STEP : (g + 1) * STEP])):
                x_s[r, pl.ds(c * WIDE + g * 8 + k, 2 * OWN, stride=PITCH), :] = v
        return carry

    lax.fori_loop(0, PEERS, spread, 0)
    lane = lax.broadcasted_iota(jnp.int32, (FULL, 128), 1)

    def matrix(t):
        parts = [jnp.where(lane < TALL, x_s[r, t * PITCH : t * PITCH + FULL, :], 0.0) for r in range(ROWS)]
        return jnp.concatenate(parts, axis=1)

    for h in range(OWN):
        left = matrix(h).astype(bf16)
        right = matrix(OWN + h)
        l_ref[h] = left
        r_ref[h] = right.astype(bf16)
        product = mm(right.T.astype(bf16), left, 1, 0)
        for r in range(ROWS):
            p_s[r, h * JPITCH : h * JPITCH + ROWS * 128, :] = product[:, r * 128 : (r + 1) * 128]

    def gather(s, carry):
        r, c = peers_of(s)
        first = (c >> 1) * 128 + (c & 1) * WIDE
        for g in range(STEPS):
            pieces = [p_s[r, pl.ds(first + g * 8 + k, OWN, stride=JPITCH), :] for k in range(8)]
            z_ref[s, :, g * STEP : (g + 1) * STEP] = fold(pieces).astype(bf16)
        return carry

    lax.fori_loop(0, PEERS, gather, 0)


def k3(z_ref, do_ref, e_ref, og_ref, ob_ref, ow_ref, dp_ref, dg_ref, gow_ref, gv_ref, z_s, owt_s, v_s):
    g = pl.program_id(0)

    @pl.when(g == 0)
    def _():
        owt_s[...] = ow_ref[...].astype(f32).T.astype(bf16)
        v_s[0] = column(og_ref[...])
        v_s[1] = column(ob_ref[...])
        gow_ref[...] = jnp.zeros_like(gow_ref)
        gv_ref[...] = jnp.zeros_like(gv_ref)

    for d in range(PEERS):
        z_s[d * OWN : (d + 1) * OWN, :] = z_ref[d].astype(f32)
    hat, inverse = hat_of(z_s[...])
    gain = wide(v_s[0])
    tri = (hat * gain + wide(v_s[1])).astype(bf16)
    d_out = do_ref[...]
    out_value = mm(owt_s[...], tri, 1, 0)
    dg_ref[...] = (e_ref[...] * out_value).astype(bf16)
    gow_ref[...] += mm(tri, d_out, 1, 1)
    up = mm(ow_ref[...], d_out, 1, 0)
    uh = up * hat
    gv_ref[0] += lane_fold(uh)
    gv_ref[1] += lane_fold(up)
    scaled = up * gain
    m1 = jnp.mean(scaled, axis=0, keepdims=True)
    m2 = jnp.mean(uh * gain, axis=0, keepdims=True)
    z_s[...] = inverse * (scaled - m1 - hat * m2)
    for d in range(PEERS):
        dp_ref[d] = z_s[d * OWN : (d + 1) * OWN, :].astype(bf16)


def k4(dp_ref, l_ref, r_ref, a_ref, x_s, o_s):
    zero = jnp.zeros((128 - TALL, 128), f32)
    for r in range(ROWS):
        for h in range(OWN):
            for q in range(ROWS):
                at = h * JPITCH + q * 128 + TALL
                x_s[r, at : at + 128 - TALL, :] = zero

    def spread(s, carry):
        r, c = peers_of(s)
        first = (c >> 1) * 128 + (c & 1) * WIDE
        rows = dp_ref[s].astype(f32)
        for g in range(STEPS):
            for k, v in enumerate(unfold(rows[:, g * STEP : (g + 1) * STEP])):
                x_s[r, pl.ds(first + g * 8 + k, OWN, stride=JPITCH), :] = v
        return carry

    lax.fori_loop(0, PEERS, spread, 0)
    lane = lax.broadcasted_iota(jnp.int32, (ROWS * 128, 128), 1)
    for h in range(OWN):
        parts = []
        for r in range(ROWS):
            x = x_s[r, h * JPITCH : h * JPITCH + ROWS * 128, :]
            parts.append(jnp.where(lane < TALL, x, 0.0).astype(bf16))
        dp = jnp.concatenate(parts, axis=1)
        d_left = mm(r_ref[h], dp, 1, 0)
        d_right = mm(l_ref[h], dp, 1, 1)
        for r in range(ROWS):
            o_s[r, h * PITCH : h * PITCH + FULL, :] = d_left[:, r * 128 : (r + 1) * 128]
            at = (OWN + h) * PITCH
            o_s[r, at : at + FULL, :] = d_right[:, r * 128 : (r + 1) * 128]

    def gather(s, carry):
        r, c = peers_of(s)
        for g in range(STEPS):
            pieces = [o_s[r, pl.ds(c * WIDE + g * 8 + k, 2 * OWN, stride=PITCH), :] for k in range(8)]
            a_ref[s, :, g * STEP : (g + 1) * STEP] = fold(pieces).astype(bf16)
        return carry

    lax.fori_loop(0, PEERS, gather, 0)


def k5(
    lim_ref, pair_ref, a_ref, dg_ref, ig_ref, ib_ref, w_ref, gw_ref, gow_ref, gv_ref,
    gp_ref, s_ref, wg_s, wv_s, bk_s, v_s, ag_s, av_s, aw_s, ai_s, pk_s,
):
    g = pl.program_id(0)

    @pl.when(g == 0)
    def _():
        perm = interleave()
        w = w_ref[...]
        gates = jnp.concatenate([w[:, :CH], w[:, 2 * CH : 3 * CH]], axis=1)
        values = jnp.concatenate([w[:, CH : 2 * CH], w[:, 3 * CH :]], axis=1)
        wg_s[...] = mm(perm, gates, 1, 1).astype(bf16)
        wv_s[...] = mm(perm, values, 1, 1).astype(bf16)
        bk_s[:, : 2 * CH] = mm(gates, perm, 1, 1).astype(bf16)
        bk_s[:, 2 * CH : 4 * CH] = mm(values, perm, 1, 1).astype(bf16)
        bk_s[:, 4 * CH :] = gw_ref[...]
        v_s[0] = column(ig_ref[...])
        v_s[1] = column(ib_ref[...])
        ag_s[...] = jnp.zeros_like(ag_s)
        av_s[...] = jnp.zeros_like(av_s)
        aw_s[...] = jnp.zeros_like(aw_s)
        ai_s[...] = jnp.zeros_like(ai_s)

    hat, inverse = hat_of(turned(pair_ref))
    gain = wide(v_s[0])
    normed = (hat * gain + wide(v_s[1])).astype(bf16)
    live = live_cells(lim_ref, g)
    d = a_ref[...].reshape(2 * CH, STEP).astype(f32) * live
    sig = sigmoid(mm(wg_s[...], normed, 1, 0))
    d_value = d * sig
    d_pre = (d_value * mm(wv_s[...], normed, 1, 0) * (1.0 - sig)).astype(bf16)
    d_value = d_value.astype(bf16)
    d_gate = dg_ref[...]
    ag_s[...] += mm(normed, d_pre, 1, 1)
    av_s[...] += mm(normed, d_value, 1, 1)
    aw_s[...] += mm(normed, d_gate, 1, 1)
    d_normed = mm(bk_s[...], jnp.concatenate([d_pre, d_value, d_gate], axis=0), 1, 0)
    dh = d_normed * hat
    ai_s[0] += lane_fold(dh)
    ai_s[1] += lane_fold(d_normed)
    scaled = d_normed * gain
    m1 = jnp.mean(scaled, axis=0, keepdims=True)
    m2 = jnp.mean(dh * gain, axis=0, keepdims=True)
    back = (inverse * (scaled - m1 - hat * m2)).T
    flat = gp_ref.reshape(STEP, CH)
    for k in range(8):
        flat[pl.ds(k, TALL, stride=8), :] = back[k * TALL : (k + 1) * TALL, :]

    @pl.when(g == STEPS - 1)
    def _():
        perm = interleave()
        gates = mm(ag_s[...].astype(bf16), perm, 1, 0)
        values = mm(av_s[...].astype(bf16), perm, 1, 0)
        lane = lax.broadcasted_iota(jnp.int32, (CH, CH), 1)
        sums = jnp.zeros((CH, CH), f32)
        for n, part in enumerate((ai_s[0], ai_s[1], gv_ref[0], gv_ref[1])):
            sums = jnp.where(lane == n, jnp.sum(part, axis=1, keepdims=True), sums)
        planes = (
            gates[:, :CH], values[:, :CH], gates[:, CH:], values[:, CH:], aw_s[...], gow_ref[...], sums,
        )
        for n, plane in enumerate(planes):
            pk_s[pl.ds(n, CH, stride=8), :] = plane
        pk_s[pl.ds(7, CH, stride=8), :] = jnp.zeros((CH, CH), f32)
        s_ref[...] = pk_s[...].astype(bf16).reshape(CH, 8, CH)


def k6(x_ref, o_ref):
    total = jnp.sum(x_ref[...].astype(f32), axis=0).astype(bf16)
    o_ref[...] = jnp.broadcast_to(total[None], o_ref.shape)


def k7(x_ref, gp_ref, gg_ref, gow_ref, gv_ref, s_s, *, factor):
    s_s[...] = x_ref[...].astype(f32).reshape(CH * 8, CH) * factor
    for q in range(4):
        gp_ref[:, q * CH : (q + 1) * CH] = s_s[pl.ds(q, CH, stride=8), :]
    gg_ref[...] = s_s[pl.ds(4, CH, stride=8), :]
    gow_ref[...] = s_s[pl.ds(5, CH, stride=8), :]
    gv_ref[...] = s_s[pl.ds(6, CH, stride=8), :].T[:8]


def whole(*shape):
    return pl.BlockSpec(shape, lambda g: (0,) * len(shape))


def tile():
    return pl.BlockSpec((TALL, 8, CH), lambda g: (0, g, 0))


def lanes(*shape):
    return pl.BlockSpec((*shape, STEP), lambda g: (0,) * len(shape) + (g,))


SMEM = pl.BlockSpec(memory_space=pltpu.SMEM)


def out(shape, dtype):
    return jax.ShapeDtypeStruct(shape, dtype)


def per_device(
    pair,
    cotangent,
    crop_length,
    in_gain,
    in_bias,
    proj_weight,
    gate_weight,
    out_gain,
    out_bias,
    out_weight,
):
    group = ("row", "col")
    everyone = ("samp", "row", "col")
    swap = functools.partial(lax.all_to_all, split_axis=0, concat_axis=0, tiled=True)
    limits = jnp.stack(
        [crop_length[0] - lax.axis_index("row") * TALL, crop_length[0] - lax.axis_index("col") * WIDE]
    )
    row = lambda v: v.reshape(1, CH)
    vm = lambda *s, dtype=f32: pltpu.VMEM(s, dtype)
    factors, d_out, slope = pl.pallas_call(
        k1,
        name="factors",
        grid=(STEPS,),
        in_specs=[SMEM, tile(), tile(), whole(1, CH), whole(1, CH), whole(CH, 4 * CH), whole(CH, CH)],
        out_specs=[lanes(PEERS, 2 * OWN), lanes(CH), lanes(CH)],
        out_shape=[out((PEERS, 2 * OWN, CELLS), bf16), out((CH, CELLS), bf16), out((CH, CELLS), f32)],
        scratch_shapes=[
            vm(2 * CH, CH, dtype=bf16), vm(2 * CH, CH, dtype=bf16), vm(CH, CH, dtype=bf16), vm(2, CH, CH),
        ],
    )(limits, pair[0], cotangent[0], row(in_gain), row(in_bias), proj_weight, gate_weight)
    factors = swap(factors, group)
    left, right, product = pl.pallas_call(
        k2,
        name="product",
        out_shape=[out((OWN, FULL, ROWS * 128), bf16)] * 2 + [out((PEERS, OWN, CELLS), bf16)],
        scratch_shapes=[vm(ROWS, 2 * OWN * PITCH, 128), vm(ROWS, OWN * JPITCH, 128)],
    )(factors)
    product = swap(product, group)
    d_product, d_gate, g_out_weight, g_out = pl.pallas_call(
        k3,
        name="middle",
        grid=(STEPS,),
        in_specs=[lanes(PEERS, OWN), lanes(CH), lanes(CH), whole(1, CH), whole(1, CH), whole(CH, CH)],
        out_specs=[lanes(PEERS, OWN), lanes(CH), whole(CH, CH), whole(2, CH, CH)],
        out_shape=[
            out((PEERS, OWN, CELLS), bf16), out((CH, CELLS), bf16), out((CH, CH), f32), out((2, CH, CH), f32),
        ],
        scratch_shapes=[vm(CH, STEP), vm(CH, CH, dtype=bf16), vm(2, CH, CH)],
    )(product, d_out, slope, row(out_gain), row(out_bias), out_weight)
    d_product = swap(d_product, group)
    d_factors = pl.pallas_call(
        k4,
        name="slopes",
        out_shape=out((PEERS, 2 * OWN, CELLS), bf16),
        scratch_shapes=[vm(ROWS, OWN * JPITCH, 128), vm(ROWS, 2 * OWN * PITCH, 128)],
    )(d_product, left, right)
    d_factors = swap(d_factors, group)
    grad_pair, packed = pl.pallas_call(
        k5,
        name="inputs",
        grid=(STEPS,),
        in_specs=[
            SMEM, tile(), lanes(PEERS, 2 * OWN), lanes(CH), whole(1, CH), whole(1, CH),
            whole(CH, 4 * CH), whole(CH, CH), whole(CH, CH), whole(2, CH, CH),
        ],
        out_specs=[tile(), whole(CH, 8, CH)],
        out_shape=[out((TALL, WIDE, CH), f32), out((CH, 8, CH), bf16)],
        scratch_shapes=[
            vm(2 * CH, CH, dtype=bf16), vm(2 * CH, CH, dtype=bf16), vm(CH, 5 * CH, dtype=bf16), vm(2, CH, CH),
            vm(CH, 2 * CH), vm(CH, 2 * CH), vm(CH, CH), vm(2, CH, CH), vm(CH * 8, CH),
        ],
    )(limits, pair[0], d_factors, d_gate, row(in_gain), row(in_bias), proj_weight, gate_weight,
      g_out_weight, g_out)
    parts = swap(packed, everyone)
    total = pl.pallas_call(k6, name="total", out_shape=out((CH, 8, CH), bf16))(parts)
    total = swap(total, everyone)
    g_proj_weight, g_gate_weight, g_out_weight, sums = pl.pallas_call(
        functools.partial(k7, factor=1.0 / FULL),
        name="unpack",
        out_shape=[out((CH, 4 * CH), f32), out((CH, CH), f32), out((CH, CH), f32), out((8, CH), f32)],
        scratch_shapes=[vm(CH * 8, CH)],
    )(total)
    return (
        grad_pair[None],
        sums[0],
        sums[1],
        g_proj_weight,
        g_gate_weight,
        sums[2],
        sums[3],
        g_out_weight,
    )


def solution(mesh):
    return jax.shard_map(
        per_device,
        mesh=mesh,
        in_specs=(
            P("samp", "row", "col", None),
            P("samp", "row", "col", None),
            P("samp"),
            P(),
            P(),
            P(),
            P(),
            P(),
            P(),
            P(),
        ),
        out_specs=(P("samp", "row", "col", None), P(), P(), P(), P(), P(), P(), P()),
        check_vma=False,
    )
```

time: 553 us -> 185 us (0.33)
  waiting for transfers between devices: 397 us -> 0 us
  blocking collectives: 0 us -> 134 us
  local copies, waits for them, and re-layouts: 62.9 us -> 1.35 us
  Pallas kernels: 0 us -> 46.3 us
  matrix products: 35.3 us -> 0 us
  other arithmetic: 30.6 us -> 0.59 us
  between operations: 15 us -> 1.29 us
  starting transfers between devices: 11.1 us -> 0 us
    all_gather x3 -> x0, waiting for transfers between devices: 200 us -> none  [the longest x1 120 us: per_device(): grad_full = lax.all_gather(d_product, 'col', axis=1, tiled=True)]
    psum x1 -> x0, waiting for transfers between devices: 139 us -> none  [packed_total(): subtotal = lax.psum(line, axis)]
    all_to_all x0 -> x6, blocking collectives: none -> 134 us  [the longest x1 31.1 us: per_device(): factors = swap(factors, group)]
    pallas_call x0 -> x7, Pallas kernels: none -> 46.3 us  [the longest x1 10.8 us: per_device(): pl.pallas_call(k4, name='slopes', out_shape=out((PEERS, 2 * OWN, CELLS),...]
    all_to_all x2 -> x0, waiting for transfers between devices: 43.2 us -> none  [cut_exchange(): lax.all_to_all(share, axis, split_axis=0, concat_axis=0, tiled=True)]
    dot_general x12 -> x0, matrix products: 35.3 us -> none  [the longest x1 9.21 us: per_device(): jnp.einsum('ijh,ikh->jkh', grad_full, left_factor, preferred_element_type...]
    all_gather x2 -> x0, local copies, waits for them, and re-layouts: 19.3 us -> none  [the longest x1 14.4 us: per_device(): left_rows = lax.all_gather(left_factor, 'col', axis=1, tiled=True)]
    reduce_scatter x1 -> x0, waiting for transfers between devices: 14.1 us -> none  [per_device(): lax.psum_scatter(jnp.einsum('ijh,ikh->jkh', grad_full, left_factor, prefe...]
  transfers between devices with their start and end apart: 7 -> 0, of which waited for: 7 -> 0; matrix products, arithmetic and copies ran while one was open for 9% -> 0% of each run, Pallas kernels for 0% -> 0%
where the time goes in v1:
time: 185 us; the launch traced here: 184 us
  blocking collectives  134 us (72%)
  Pallas kernels  46.3 us (25%)
    all_to_all x1, blocking collectives, per_device(): factors = swap(factors, group)  31.1 us
    all_to_all x1, blocking collectives, per_device(): d_factors = swap(d_factors, group)  28.7 us
    all_to_all x1, blocking collectives, per_device(): d_product = swap(d_product, group)  19.5 us
    all_to_all x1, blocking collectives, per_device(): product = swap(product, group)  19.5 us
    all_to_all x1, blocking collectives, per_device(): parts = swap(packed, everyone)  19.4 us
    all_to_all x1, blocking collectives, per_device(): total = swap(total, everyone)  16.1 us
    pallas_call x1, Pallas kernels, per_device(): pl.pallas_call(k4, name='slopes', out_shape=out((PEERS, 2 * OWN, CELLS),...  10.8 us
    pallas_call x1, Pallas kernels, per_device(): pl.pallas_call(k2, name='product', out_shape=[out((OWN, FULL, ROWS * 128)...  10.4 us

profile of v1, /device:TPU:1, one launch (start us, length us, event | category | flops | bytes accessed | tf_op | source)
XLA Modules:
  0.0 183.7 jit_solution(18132465527639879734)
XLA Ops:
  1.3 0.6 pad_add_fusion.lim_ref
  1.9 6.8 %factors.1 = (bf16[32,8,3200]{2,1,0:T(8,128)(2,1)}, bf16[128,3200]{1,0:T(8,128)(2,1)}, f32[128,3200]{1,0:T(8,128)}) custom-call(s32[2]{0:T(128)} %pad_add_fusion.lim_ref, f32[80,40,128]{2,1,0:T(8,128)} %bitcast.20, f32[80,40,128]{2,1,0:T(8,128)} %bitcast.22, f32[1,128]{1,0:T(1,128)} %bitcast.23, f32[1,128]{1,0:T(1,128)} %bitcast.25, bf16[128,512]{1,0:T(8,128)(2,1)} %w_ref.3, ...), custom_call_target="tpu_custom_call" | custom-call | tf_op jit(solution)/shard_map/factors/pallas_call | solution.py:375
  8.7 31.1 %all_to_all.30.y_ref = bf16[32,8,3200]{2,1,0:T(8,128)(2,1)} all-to-all(bf16[32,8,3200]{2,1,0:T(8,128)(2,1)} %get-tuple-element.24), channel_id=1, replica_groups=mesh['samp'=4,'row'=4,'col'=8] {'row','col'}, dimensions={0} | all-to-all | bytes 3276800 | tf_op jit(solution)/shard_map/all_to_all | solution.py:386
  39.8 10.4 %product.1 = (bf16[4,320,512]{2,1,0:T(8,128)(2,1)}, bf16[4,320,512]{2,1,0:T(8,128)(2,1)}, bf16[32,4,3200]{2,1,0:T(4,128)(2,1)}) custom-call(bf16[32,8,3200]{2,1,0:T(8,128)(2,1)} %all_to_all.30.y_ref), custom_call_target="tpu_custom_call" | custom-call | tf_op jit(solution)/shard_map/product/pallas_call | solution.py:387
  50.2 19.5 %all_to_all.31.z_ref = bf16[32,4,3200]{2,1,0:T(4,128)(2,1)} all-to-all(bf16[32,4,3200]{2,1,0:T(4,128)(2,1)} %get-tuple-element.25), channel_id=1, replica_groups=mesh['samp'=4,'row'=4,'col'=8] {'row','col'}, dimensions={0} | all-to-all | bytes 1638400 | tf_op jit(solution)/shard_map/all_to_all | solution.py:393
  69.7 6.1 %middle.1 = (bf16[32,4,3200]{2,1,0:T(4,128)(2,1)}, bf16[128,3200]{1,0:T(8,128)(2,1)}, f32[128,128]{1,0:T(8,128)}, f32[2,128,128]{2,1,0:T(8,128)}) custom-call(bf16[32,4,3200]{2,1,0:T(4,128)(2,1)} %all_to_all.31.z_ref, bf16[128,3200]{1,0:T(8,128)(2,1)} %get-tuple-element.26.do_ref, f32[128,3200]{1,0:T(8,128)} %get-tuple-element.27.e_ref, f32[1,128]{1,0:T(1,128)} %bitcast.27, ...), custom_call_target="tpu_custom_call" | custom-call | tf_op jit(solution)/shard_map/middle/pallas_call | solution.py:394
  75.7 19.5 %all_to_all.32.dp_ref = bf16[32,4,3200]{2,1,0:T(4,128)(2,1)} all-to-all(bf16[32,4,3200]{2,1,0:T(4,128)(2,1)} %get-tuple-element.28), channel_id=1, replica_groups=mesh['samp'=4,'row'=4,'col'=8] {'row','col'}, dimensions={0} | all-to-all | bytes 1638400 | tf_op jit(solution)/shard_map/all_to_all | solution.py:405
  95.3 10.8 %slopes.1 = bf16[32,8,3200]{2,1,0:T(8,128)(2,1)} custom-call(bf16[32,4,3200]{2,1,0:T(4,128)(2,1)} %all_to_all.32.dp_ref, bf16[4,320,512]{2,1,0:T(8,128)(2,1)} %get-tuple-element.29.l_ref, bf16[4,320,512]{2,1,0:T(8,128)(2,1)} %get-tuple-element.30.r_ref), custom_call_target="tpu_custom_call" | custom-call | tf_op jit(solution)/shard_map/slopes/pallas_call | solution.py:406
  106.1 28.7 %all_to_all.33.a_ref = bf16[32,8,3200]{2,1,0:T(8,128)(2,1)} all-to-all(bf16[32,8,3200]{2,1,0:T(8,128)(2,1)} %slopes.1), channel_id=1, replica_groups=mesh['samp'=4,'row'=4,'col'=8] {'row','col'}, dimensions={0} | all-to-all | bytes 3276800 | tf_op jit(solution)/shard_map/all_to_all | solution.py:412
  134.7 8.6 %inputs.1 = (f32[80,40,128]{2,1,0:T(8,128)}, bf16[128,8,128]{2,1,0:T(8,128)(2,1)}) custom-call(s32[2]{0:T(128)} %pad_add_fusion.lim_ref, f32[80,40,128]{2,1,0:T(8,128)} %bitcast.21, bf16[32,8,3200]{2,1,0:T(8,128)(2,1)} %all_to_all.33.a_ref, bf16[128,3200]{1,0:T(8,128)(2,1)} %get-tuple-element.31.dg_ref, f32[1,128]{1,0:T(1,128)} %bitcast.24, ...), custom_call_target="tpu_custom_call" | custom-call | tf_op jit(solution)/shard_map/inputs/pallas_call | solution.py:413
  143.3 19.4 %all_to_all.34.x_ref = bf16[128,8,128]{2,1,0:T(8,128)(2,1)} all-to-all(bf16[128,8,128]{2,1,0:T(8,128)(2,1)} %get-tuple-element.35), channel_id=1, replica_groups=mesh['samp'=4,'row'=4,'col'=8] {'samp','row','col'}, dimensions={0} | all-to-all | bytes 524288 | tf_op jit(solution)/shard_map/all_to_all | solution.py:429
  162.7 1.8 total.1
  164.5 16.1 %all_to_all.35.x_ref = bf16[128,8,128]{2,1,0:T(8,128)(2,1)} all-to-all(bf16[128,8,128]{2,1,0:T(8,128)(2,1)} %total.1), channel_id=1, replica_groups=mesh['samp'=4,'row'=4,'col'=8] {'samp','row','col'}, dimensions={0} | all-to-all | bytes 524288 | tf_op jit(solution)/shard_map/all_to_all | solution.py:431
  180.5 1.8 unpack.1
  182.4 1.3 slice_bitcast_fusion

commit v2 on v1

v2 whole, which is shorter than its diff:
```python
import functools

import jax
import jax.numpy as jnp
from jax import lax
from jax.experimental import pallas as pl
from jax.experimental.pallas import tpu as pltpu
from jax.sharding import PartitionSpec as P

epsilon = 1e-05

TALL = 80
WIDE = 40
CH = 128
ROWS = 4
COLS = 8
PEERS = ROWS * COLS
OWN = CH // PEERS
CELLS = TALL * WIDE
STEP = 8 * TALL
STEPS = CELLS // STEP
FULL = COLS * WIDE
PITCH = FULL + 8
JPITCH = ROWS * 128 + 8
f32 = jnp.float32
bf16 = jnp.bfloat16


def mm(a, b, ca, cb):
    return lax.dot_general(a, b, (((ca,), (cb,)), ((), ())), preferred_element_type=f32)


def sigmoid(x):
    return 0.5 * jnp.tanh(0.5 * x) + 0.5


def column(row):
    return jnp.broadcast_to(row, (CH, CH)).T


def wide(col):
    return jnp.concatenate([col] * (STEP // CH), axis=1)


def interleave():
    n = 2 * CH
    q = lax.broadcasted_iota(jnp.int32, (n, n), 0)
    p = lax.broadcasted_iota(jnp.int32, (n, n), 1)
    src = ((q >> 2) & 1) * CH + (q >> 3) * OWN + (q & 3)
    return jnp.where(src == p, 1.0, 0.0).astype(bf16)


def turned(ref):
    flat = ref.reshape(STEP, CH)
    rows = [flat[pl.ds(k, TALL, stride=8), :] for k in range(8)]
    return jnp.concatenate(rows, axis=0).T


def live_cells(crop_ref, g):
    lane = lax.broadcasted_iota(jnp.int32, (1, STEP), 1)
    k = jnp.zeros((1, STEP), jnp.int32)
    for m in range(1, 8):
        k = k + jnp.where(lane >= m * TALL, 1, 0)
    i = lane - k * TALL + lax.axis_index("row") * TALL
    k = k + (g * 8 + lax.axis_index("col") * WIDE)
    live = jnp.logical_and(i < crop_ref[0], k < crop_ref[0])
    return jnp.where(live, 1.0, 0.0).astype(f32)


def hat_of(x):
    centre = jnp.mean(x, axis=0, keepdims=True)
    centered = x - centre
    inverse = lax.rsqrt(jnp.mean(centered * centered, axis=0, keepdims=True) + epsilon)
    return centered * inverse, inverse


def lane_fold(x):
    out = x[:, :CH]
    for m in range(1, x.shape[1] // CH):
        out = out + x[:, m * CH : (m + 1) * CH]
    return out


def peers_of(s):
    return s >> 3, s & 7


def unfold(rows):
    n = rows.shape[0]
    lane = lax.broadcasted_iota(jnp.int32, (n, 128), 1)
    out = []
    for k in range(8):
        at = k * TALL
        m, off = at // 128, at % 128
        v = rows[:, m * 128 : (m + 1) * 128]
        if off + TALL > 128:
            v = jnp.where(lane >= off, v, rows[:, (m + 1) * 128 : (m + 2) * 128])
        out.append(pltpu.roll(v, 128 - off, 1) if off else v)
    return out


def fold(pieces):
    n = pieces[0].shape[0]
    lane = lax.broadcasted_iota(jnp.int32, (n, 128), 1)
    r = [pltpu.roll(p, (k * TALL) % 128, 1) if k else p for k, p in enumerate(pieces)]
    cols = []
    for m in range(STEP // 128):
        lo, hi = m * 128, (m + 1) * 128
        v = None
        for k in range(8):
            a, b = max(lo, k * TALL), min(hi, (k + 1) * TALL)
            if a >= b:
                continue
            v = r[k] if v is None else jnp.where(lane >= a - lo, r[k], v)
        cols.append(v)
    return jnp.concatenate(cols, axis=1)


def sides(w):
    gates = jnp.concatenate([w[:, :CH], w[:, 2 * CH : 3 * CH]], axis=1)
    values = jnp.concatenate([w[:, CH : 2 * CH], w[:, 3 * CH :]], axis=1)
    return gates, values


def gathered(gather, buf, ref, sem):
    part = PEERS // 4
    copies = []
    for q in range(4):
        lax.fori_loop(q * part, (q + 1) * part, gather, 0, unroll=8)
        if q:
            copies[-1].start()
        rows = pl.ds(q * part, part)
        copies.append(pltpu.make_async_copy(buf.at[rows], ref.at[rows], sem.at[q]))
    copies[-1].start()
    return copies


def k1(crop_ref, pair_ref, ig_ref, ib_ref, w_ref, f_ref, wg_s, wv_s, v_s):
    g = pl.program_id(0)

    @pl.when(g == 0)
    def _():
        perm = interleave()
        gates, values = sides(w_ref[...])
        wg_s[...] = mm(perm, gates, 1, 1).astype(bf16)
        wv_s[...] = mm(perm, values, 1, 1).astype(bf16)
        v_s[0] = column(ig_ref[...])
        v_s[1] = column(ib_ref[...])

    hat, _ = hat_of(turned(pair_ref))
    normed = (hat * wide(v_s[0]) + wide(v_s[1])).astype(bf16)
    value = mm(wv_s[...], normed, 1, 0) * live_cells(crop_ref, g)
    factor = sigmoid(mm(wg_s[...], normed, 1, 0)) * value
    f_ref[...] = factor.astype(bf16).reshape(PEERS, 2 * OWN, STEP)


def k1b(
    crop_ref, pair_ref, cot_ref, ig_ref, ib_ref, w_ref, gw_ref, n_ref, do_ref, e_ref, sv_ref, sg_ref,
    wg_s, wv_s, gw_s, v_s,
):
    g = pl.program_id(0)

    @pl.when(g == 0)
    def _():
        perm = interleave()
        gates, values = sides(w_ref[...])
        wg_s[...] = mm(perm, gates, 1, 1).astype(bf16)
        wv_s[...] = mm(perm, values, 1, 1).astype(bf16)
        gw_s[...] = gw_ref[...].astype(f32).T.astype(bf16)
        v_s[0] = column(ig_ref[...])
        v_s[1] = column(ib_ref[...])

    hat, _ = hat_of(turned(pair_ref))
    normed = (hat * wide(v_s[0]) + wide(v_s[1])).astype(bf16)
    n_ref[:CH, :] = normed
    n_ref[CH:, :] = jnp.ones((16, STEP), bf16)
    sig = sigmoid(mm(wg_s[...], normed, 1, 0))
    live_sig = sig * live_cells(crop_ref, g)
    sv_ref[...] = live_sig.astype(bf16)
    sg_ref[...] = (live_sig * mm(wv_s[...], normed, 1, 0) * (1.0 - sig)).astype(bf16)
    gate = sigmoid(mm(gw_s[...], normed, 1, 0))
    up = turned(cot_ref) * gate
    do_ref[...] = up.astype(bf16)
    e_ref[...] = up * (1.0 - gate)


def k2(y_ref, l_ref, r_ref, z_ref, x_s, p_s, l_s, r_s, z_s, sem, z_sem):
    def spread(s, carry):
        r, c = peers_of(s)
        rows = y_ref[s].astype(f32)
        for g in range(STEPS):
            for k, v in enumerate(unfold(rows[:, g * STEP : (g + 1) * STEP])):
                x_s[r, pl.ds(c * WIDE + g * 8 + k, 2 * OWN, stride=PITCH), :] = v
        return carry

    lax.fori_loop(0, PEERS, spread, 0, unroll=8)
    lane = lax.broadcasted_iota(jnp.int32, (FULL, 128), 1)

    def matrix(t):
        parts = [jnp.where(lane < TALL, x_s[r, t * PITCH : t * PITCH + FULL, :], 0.0) for r in range(ROWS)]
        return jnp.concatenate(parts, axis=1)

    for h in range(OWN):
        left = matrix(h).astype(bf16)
        right = matrix(OWN + h)
        l_s[h] = left
        r_s[h] = right.astype(bf16)
        product = mm(right.T.astype(bf16), left, 1, 0)
        for r in range(ROWS):
            p_s[r, h * JPITCH : h * JPITCH + ROWS * 128, :] = product[:, r * 128 : (r + 1) * 128]

    copies = [pltpu.make_async_copy(l_s, l_ref, sem.at[0]), pltpu.make_async_copy(r_s, r_ref, sem.at[1])]
    for copy in copies:
        copy.start()

    def gather(s, carry):
        r, c = peers_of(s)
        first = (c >> 1) * 128 + (c & 1) * WIDE
        for g in range(STEPS):
            pieces = [p_s[r, pl.ds(first + g * 8 + k, OWN, stride=JPITCH), :] for k in range(8)]
            z_s[s, :, g * STEP : (g + 1) * STEP] = fold(pieces).astype(bf16)
        return carry

    for copy in copies + gathered(gather, z_s, z_ref, z_sem):
        copy.wait()


def k3(z_ref, do_ref, og_ref, ow_ref, dp_ref, z_s, v_s):
    @pl.when(pl.program_id(0) == 0)
    def _():
        v_s[...] = column(og_ref[...])

    for d in range(PEERS):
        z_s[d * OWN : (d + 1) * OWN, :] = z_ref[d].astype(f32)
    hat, inverse = hat_of(z_s[...])
    scaled = mm(ow_ref[...], do_ref[...], 1, 0) * wide(v_s[...])
    m1 = jnp.mean(scaled, axis=0, keepdims=True)
    m2 = jnp.mean(scaled * hat, axis=0, keepdims=True)
    z_s[...] = inverse * (scaled - m1 - hat * m2)
    for d in range(PEERS):
        dp_ref[d] = z_s[d * OWN : (d + 1) * OWN, :].astype(bf16)


def k3b(
    z_ref, n_ref, do_ref, e_ref, og_ref, ob_ref, ow_ref, dg_ref, gow_ref, gv_ref, gg_ref,
    z_s, owt_s, v_s,
):
    @pl.when(pl.program_id(0) == 0)
    def _():
        owt_s[...] = ow_ref[...].astype(f32).T.astype(bf16)
        v_s[0] = column(og_ref[...])
        v_s[1] = column(ob_ref[...])
        gow_ref[...] = jnp.zeros_like(gow_ref)
        gv_ref[...] = jnp.zeros_like(gv_ref)
        gg_ref[...] = jnp.zeros_like(gg_ref)

    for d in range(PEERS):
        z_s[d * OWN : (d + 1) * OWN, :] = z_ref[d].astype(f32)
    hat, _ = hat_of(z_s[...])
    tri = (hat * wide(v_s[0]) + wide(v_s[1])).astype(bf16)
    d_out = do_ref[...]
    d_gate = (e_ref[...] * mm(owt_s[...], tri, 1, 0)).astype(bf16)
    dg_ref[...] = d_gate
    gow_ref[...] += mm(tri, d_out, 1, 1)
    gg_ref[...] += mm(n_ref[...], d_gate, 1, 1)
    up = mm(ow_ref[...], d_out, 1, 0)
    gv_ref[0] += lane_fold(up * hat)
    gv_ref[1] += lane_fold(up)


def k4(dp_ref, l_ref, r_ref, a_ref, x_s, o_s, a_s, sem):
    zero = jnp.zeros((128 - TALL, 128), f32)
    for r in range(ROWS):
        for h in range(OWN):
            for q in range(ROWS):
                at = h * JPITCH + q * 128 + TALL
                x_s[r, at : at + 128 - TALL, :] = zero

    def spread(s, carry):
        r, c = peers_of(s)
        first = (c >> 1) * 128 + (c & 1) * WIDE
        rows = dp_ref[s].astype(f32)
        for g in range(STEPS):
            for k, v in enumerate(unfold(rows[:, g * STEP : (g + 1) * STEP])):
                x_s[r, pl.ds(first + g * 8 + k, OWN, stride=JPITCH), :] = v
        return carry

    lax.fori_loop(0, PEERS, spread, 0, unroll=8)
    lane = lax.broadcasted_iota(jnp.int32, (ROWS * 128, 128), 1)
    for h in range(OWN):
        parts = []
        for r in range(ROWS):
            x = x_s[r, h * JPITCH : h * JPITCH + ROWS * 128, :]
            parts.append(jnp.where(lane < TALL, x, 0.0).astype(bf16))
        dp = jnp.concatenate(parts, axis=1)
        d_left = mm(r_ref[h], dp, 1, 0)
        d_right = mm(l_ref[h], dp, 1, 1)
        for r in range(ROWS):
            o_s[r, h * PITCH : h * PITCH + FULL, :] = d_left[:, r * 128 : (r + 1) * 128]
            at = (OWN + h) * PITCH
            o_s[r, at : at + FULL, :] = d_right[:, r * 128 : (r + 1) * 128]

    def gather(s, carry):
        r, c = peers_of(s)
        for g in range(STEPS):
            pieces = [o_s[r, pl.ds(c * WIDE + g * 8 + k, 2 * OWN, stride=PITCH), :] for k in range(8)]
            a_s[s, :, g * STEP : (g + 1) * STEP] = fold(pieces).astype(bf16)
        return carry

    for copy in gathered(gather, a_s, a_ref, sem):
        copy.wait()


def k5(
    a_ref, sv_ref, sg_ref, n_ref, ig_ref, ib_ref, w_ref, gw_ref, gow_ref, gv_ref, gg_ref,
    s_ref, ag_s, av_s, pk_s,
):
    g = pl.program_id(0)

    @pl.when(g == 0)
    def _():
        ag_s[...] = jnp.zeros_like(ag_s)
        av_s[...] = jnp.zeros_like(av_s)

    d = a_ref[...].reshape(2 * CH, STEP).astype(f32)
    normed = n_ref[...]
    ag_s[...] += mm(normed, (d * sg_ref[...].astype(f32)).astype(bf16), 1, 1)
    av_s[...] += mm(normed, (d * sv_ref[...].astype(f32)).astype(bf16), 1, 1)

    @pl.when(g == STEPS - 1)
    def _():
        perm = interleave()
        gates, values = sides(w_ref[...])
        weights = (mm(gates, perm, 1, 1), mm(values, perm, 1, 1), gw_ref[...].astype(f32))
        slope = jnp.zeros((CH, 1), f32)
        shift = jnp.zeros((CH, 1), f32)
        for weight, grad in zip(weights, (ag_s, av_s, gg_ref)):
            slope += jnp.sum(weight * grad[:CH, :], axis=1, keepdims=True)
            shift += jnp.sum(weight * grad[CH : CH + 1, :], axis=1, keepdims=True)
        gain, bias = column(ig_ref[...]), column(ib_ref[...])
        lane = lax.broadcasted_iota(jnp.int32, (CH, CH), 1)
        sums = jnp.where(lane == 0, (slope - bias * shift) / gain, jnp.where(lane == 1, shift, 0.0))
        for n in range(2):
            sums = jnp.where(lane == 2 + n, jnp.sum(gv_ref[n], axis=1, keepdims=True), sums)
        d_gates = mm(ag_s[:CH, :].astype(bf16), perm, 1, 0)
        d_values = mm(av_s[:CH, :].astype(bf16), perm, 1, 0)
        planes = (
            d_gates[:, :CH], d_values[:, :CH], d_gates[:, CH:], d_values[:, CH:],
            gg_ref[:CH, :], gow_ref[...], sums, jnp.zeros((CH, CH), f32),
        )
        for n, plane in enumerate(planes):
            pk_s[pl.ds(n, CH, stride=8), :] = plane
        s_ref[...] = pk_s[...].astype(bf16).reshape(CH, 8, CH)


def k5b(pair_ref, a_ref, sv_ref, sg_ref, dg_ref, ig_ref, w_ref, gw_ref, gp_ref, bk_s, v_s):
    @pl.when(pl.program_id(0) == 0)
    def _():
        perm = interleave()
        gates, values = sides(w_ref[...])
        bk_s[:, : 2 * CH] = mm(gates, perm, 1, 1).astype(bf16)
        bk_s[:, 2 * CH : 4 * CH] = mm(values, perm, 1, 1).astype(bf16)
        bk_s[:, 4 * CH :] = gw_ref[...]
        v_s[...] = column(ig_ref[...])

    hat, inverse = hat_of(turned(pair_ref))
    d = a_ref[...].reshape(2 * CH, STEP).astype(f32)
    d_gates = (d * sg_ref[...].astype(f32)).astype(bf16)
    d_values = (d * sv_ref[...].astype(f32)).astype(bf16)
    d_normed = mm(bk_s[...], jnp.concatenate([d_gates, d_values, dg_ref[...]], axis=0), 1, 0)
    scaled = d_normed * wide(v_s[...])
    m1 = jnp.mean(scaled, axis=0, keepdims=True)
    m2 = jnp.mean(scaled * hat, axis=0, keepdims=True)
    back = (inverse * (scaled - m1 - hat * m2)).T
    flat = gp_ref.reshape(STEP, CH)
    for k in range(8):
        flat[pl.ds(k, TALL, stride=8), :] = back[k * TALL : (k + 1) * TALL, :]


def k6(x_ref, o_ref):
    total = jnp.sum(x_ref[...].astype(f32), axis=0).astype(bf16)
    o_ref[...] = jnp.broadcast_to(total[None], o_ref.shape)


def k7(x_ref, gp_ref, gg_ref, gow_ref, *rest, factor):
    s_s = rest[-1]
    s_s[...] = x_ref[...].astype(f32).reshape(CH * 8, CH) * factor
    for q in range(4):
        gp_ref[:, q * CH : (q + 1) * CH] = s_s[pl.ds(q, CH, stride=8), :]
    gg_ref[...] = s_s[pl.ds(4, CH, stride=8), :]
    gow_ref[...] = s_s[pl.ds(5, CH, stride=8), :]
    sums = s_s[pl.ds(6, CH, stride=8), :].T
    for n in range(4):
        rest[n][...] = sums[n : n + 1]


def whole(*shape):
    return pl.BlockSpec(shape, lambda g: (0,) * len(shape))


def tile():
    return pl.BlockSpec((TALL, 8, CH), lambda g: (0, g, 0))


def lanes(*shape):
    return pl.BlockSpec((*shape, STEP), lambda g: (0,) * len(shape) + (g,))


SMEM = pl.BlockSpec(memory_space=pltpu.SMEM)
SMALL = pltpu.CompilerParams(vmem_limit_bytes=12 << 20)
LARGE = pltpu.CompilerParams(vmem_limit_bytes=22 << 20)
cost = pl.CostEstimate(flops=1_000_000_000, transcendentals=0, bytes_accessed=8_000_000)


def out(shape, dtype):
    return jax.ShapeDtypeStruct(shape, dtype)


def away(shape, dtype):
    return pltpu.HBM(shape, dtype)


def keep_away(*arrays):
    return [pltpu.with_memory_space_constraint(a, pltpu.HBM) for a in arrays]


def vm(*shape, dtype=f32):
    return pltpu.VMEM(shape, dtype)


def product_call(factors, name):
    return pl.pallas_call(
        k2,
        name=name,
        compiler_params=LARGE,
        out_specs=[pl.BlockSpec(memory_space=pltpu.HBM)] * 3,
        out_shape=[away((OWN, FULL, ROWS * 128), bf16)] * 2 + [away((PEERS, OWN, CELLS), bf16)],
        scratch_shapes=[
            vm(ROWS, 2 * OWN * PITCH, 128), vm(ROWS, OWN * JPITCH, 128),
            vm(OWN, FULL, ROWS * 128, dtype=bf16), vm(OWN, FULL, ROWS * 128, dtype=bf16),
            vm(PEERS, OWN, CELLS, dtype=bf16), pltpu.SemaphoreType.DMA((2,)), pltpu.SemaphoreType.DMA((4,)),
        ],
    )(factors)


def slopes_call(d_product, left, right, name):
    return pl.pallas_call(
        k4,
        name=name,
        compiler_params=LARGE,
        out_specs=pl.BlockSpec(memory_space=pltpu.HBM),
        out_shape=away((PEERS, 2 * OWN, CELLS), bf16),
        scratch_shapes=[
            vm(ROWS, OWN * JPITCH, 128), vm(ROWS, 2 * OWN * PITCH, 128),
            vm(PEERS, 2 * OWN, CELLS, dtype=bf16), pltpu.SemaphoreType.DMA((4,)),
        ],
    )(d_product, left, right)


def per_device(
    pair,
    cotangent,
    crop_length,
    in_gain,
    in_bias,
    proj_weight,
    gate_weight,
    out_gain,
    out_bias,
    out_weight,
):
    group = ("row", "col")
    everyone = ("samp", "row", "col")
    swap = functools.partial(lax.all_to_all, split_axis=0, concat_axis=0, tiled=True)
    row = lambda v: v.reshape(1, CH)
    wb = functools.partial(vm, dtype=bf16)
    pair, cotangent = pair[0], cotangent[0]
    in_gain, in_bias, out_gain, out_bias = map(row, (in_gain, in_bias, out_gain, out_bias))
    one, square, proj = whole(1, CH), whole(CH, CH), whole(CH, 4 * CH)
    both = (PEERS, 2 * OWN, CELLS)
    factors = pl.pallas_call(
        k1,
        name="factors",
        compiler_params=SMALL,
        grid=(STEPS,),
        in_specs=[SMEM, tile(), one, one, proj],
        out_specs=lanes(PEERS, 2 * OWN),
        out_shape=out(both, bf16),
        scratch_shapes=[wb(2 * CH, CH), wb(2 * CH, CH), vm(2, CH, CH)],
    )(crop_length, *keep_away(pair, in_gain, in_bias, proj_weight))
    factors = swap(factors, group)
    normed, d_out, slope, by_value, by_gate = pl.pallas_call(
        k1b,
        name="gate",
        compiler_params=SMALL,
        grid=(STEPS,),
        in_specs=[SMEM, tile(), tile(), one, one, proj, square],
        out_specs=[lanes(CH + 16), lanes(CH), lanes(CH), lanes(2 * CH), lanes(2 * CH)],
        out_shape=[
            away((CH + 16, CELLS), bf16), away((CH, CELLS), bf16), away((CH, CELLS), f32),
            away((2 * CH, CELLS), bf16), away((2 * CH, CELLS), bf16),
        ],
        scratch_shapes=[wb(2 * CH, CH), wb(2 * CH, CH), wb(CH, CH), vm(2, CH, CH)],
        cost_estimate=cost,
    )(crop_length, *keep_away(pair, cotangent, in_gain, in_bias, proj_weight, gate_weight))
    left, right, product = product_call(factors, "product")
    product = swap(product, group)
    d_product = pl.pallas_call(
        k3,
        name="middle",
        compiler_params=SMALL,
        grid=(STEPS,),
        in_specs=[lanes(PEERS, OWN), lanes(CH), one, square],
        out_specs=lanes(PEERS, OWN),
        out_shape=out((PEERS, OWN, CELLS), bf16),
        scratch_shapes=[vm(CH, STEP), vm(CH, CH)],
    )(product, *keep_away(d_out, out_gain, out_weight))
    d_product = swap(d_product, group)
    d_gate, g_out_weight, g_out, g_gate = pl.pallas_call(
        k3b,
        name="outputs",
        compiler_params=SMALL,
        grid=(STEPS,),
        in_specs=[lanes(PEERS, OWN), lanes(CH + 16), lanes(CH), lanes(CH), one, one, square],
        out_specs=[lanes(CH), square, whole(2, CH, CH), whole(CH + 16, CH)],
        out_shape=[
            away((CH, CELLS), bf16), away((CH, CH), f32), away((2, CH, CH), f32), away((CH + 16, CH), f32),
        ],
        scratch_shapes=[vm(CH, STEP), wb(CH, CH), vm(2, CH, CH)],
        cost_estimate=cost,
    )(product, *keep_away(normed, d_out, slope, out_gain, out_bias, out_weight))
    d_factors = slopes_call(d_product, left, right, "slopes")
    d_factors = swap(d_factors, group)
    packed = pl.pallas_call(
        k5,
        name="weights",
        compiler_params=SMALL,
        grid=(STEPS,),
        in_specs=[
            lanes(PEERS, 2 * OWN), lanes(2 * CH), lanes(2 * CH), lanes(CH + 16), one, one,
            proj, square, square, whole(2, CH, CH), whole(CH + 16, CH),
        ],
        out_specs=whole(CH, 8, CH),
        out_shape=out((CH, 8, CH), bf16),
        scratch_shapes=[vm(CH + 16, 2 * CH), vm(CH + 16, 2 * CH), vm(CH * 8, CH)],
    )(d_factors, *keep_away(by_value, by_gate, normed, in_gain, in_bias, proj_weight, gate_weight,
                            g_out_weight, g_out, g_gate))
    parts = swap(packed, everyone)
    grad_pair = pl.pallas_call(
        k5b,
        name="inputs",
        compiler_params=SMALL,
        grid=(STEPS,),
        in_specs=[
            tile(), lanes(PEERS, 2 * OWN), lanes(2 * CH), lanes(2 * CH), lanes(CH), one, proj, square,
        ],
        out_specs=tile(),
        out_shape=out((TALL, WIDE, CH), f32),
        scratch_shapes=[wb(CH, 5 * CH), vm(CH, CH)],
        cost_estimate=cost,
    )(*keep_away(pair), d_factors, *keep_away(by_value, by_gate, d_gate, in_gain, proj_weight, gate_weight))
    total = pl.pallas_call(k6, name="total", compiler_params=SMALL, out_shape=out((CH, 8, CH), bf16))(parts)
    total = swap(total, everyone)
    g_proj_weight, g_gate_weight, g_out_weight, *sums = pl.pallas_call(
        functools.partial(k7, factor=1.0 / FULL),
        name="unpack",
        compiler_params=SMALL,
        out_shape=[out((CH, 4 * CH), f32), out((CH, CH), f32), out((CH, CH), f32)] + [out((1, CH), f32)] * 4,
        scratch_shapes=[vm(CH * 8, CH)],
    )(total)
    sums = [s.reshape(CH) for s in sums]
    return (
        grad_pair[None],
        sums[0],
        sums[1],
        g_proj_weight,
        g_gate_weight,
        sums[2],
        sums[3],
        g_out_weight,
    )


def solution(mesh):
    return jax.shard_map(
        per_device,
        mesh=mesh,
        in_specs=(
            P("samp", "row", "col", None),
            P("samp", "row", "col", None),
            P("samp"),
            P(),
            P(),
            P(),
            P(),
            P(),
            P(),
            P(),
        ),
        out_specs=(P("samp", "row", "col", None), P(), P(), P(), P(), P(), P(), P()),
        check_vma=False,
    )
```

time: 185 us -> 157 us (0.85)
  blocking collectives: 134 us -> 68.5 us
  waiting for transfers between devices: 0 us -> 26.4 us
  starting transfers between devices: 0 us -> 15.3 us
    all_to_all x3 -> x0, blocking collectives: 64.2 us -> none  [the longest x1 28.7 us: per_device(): d_factors = swap(d_factors, group)]
    all_to_all x0 -> x3, waiting for transfers between devices: none -> 26.4 us  [the longest x1 16 us: per_device(): d_factors = swap(d_factors, group)]
    all_to_all x0 -> x3, starting transfers between devices: none -> 15.3 us  [the longest x1 5.56 us: per_device(): d_factors = swap(d_factors, group)]
    pallas_call x7 -> x10, Pallas kernels: 46.3 us -> 44.8 us  [the longest x1 7.38 us: per_device(): pl.pallas_call(k1b, name='gate', compiler_params=SMALL, grid=(STEPS,), in...]
  transfers between devices with their start and end apart: 0 -> 3, of which waited for: 0 -> 3; matrix products, arithmetic and copies ran while one was open for 0% -> 0% of each run, Pallas kernels for 0% -> 13%
where the time goes in v2:
time: 157 us; the launch traced here: 156 us
  blocking collectives  68.5 us (44%)
  Pallas kernels  44.8 us (29%)
  waiting for transfers between devices  26.4 us (17%)
  starting transfers between devices  15.3 us (10%)
    all_to_all x1, blocking collectives, per_device(): factors = swap(factors, group)  30.8 us
    all_to_all x1, blocking collectives, per_device(): parts = swap(packed, everyone)  19.2 us
    all_to_all x1, blocking collectives, per_device(): d_product = swap(d_product, group)  18.6 us
    all_to_all x1, waiting for transfers between devices, per_device(): d_factors = swap(d_factors, group)  16 us
    pallas_call x1, Pallas kernels, per_device(): pl.pallas_call(k1b, name='gate', compiler_params=SMALL, grid=(STEPS,), in...  7.38 us
    pallas_call x1, Pallas kernels, per_device(): pl.pallas_call(k5b, name='inputs', compiler_params=SMALL, grid=(STEPS,),...  6.66 us
    pallas_call x1, Pallas kernels, per_device(): pl.pallas_call(k3b, name='outputs', compiler_params=SMALL, grid=(STEPS,),...  6.13 us
    all_to_all x1, waiting for transfers between devices, per_device(): product = swap(product, group)  6 us
  transfers between devices with their start and end apart: 3, of which 3 were waited for; matrix products, arithmetic and copies ran while one was open for 0% of the time, Pallas kernels for 13%

profile of v2, /device:TPU:1, one launch (start us, length us, event | category | flops | bytes accessed | tf_op | source)
XLA Modules:
  0.0 156.5 jit_solution(7919979673637787835)
XLA Ops:
  1.3 5.0 %factors.1 = bf16[32,8,3200]{2,1,0:T(8,128)(2,1)S(1)} custom-call(s32[1]{0:T(128)S(6)} %copy.18.crop_ref, f32[80,40,128]{2,1,0:T(8,128)} %bitcast.11, f32[1,128]{1,0:T(1,128)} %bitcast.15, f32[1,128]{1,0:T(1,128)} %bitcast.19, bf16[128,512]{1,0:T(8,128)(2,1)} %w_ref.7), custom_call_target="tpu_custom_call" | custom-call | tf_op jit(solution)/shard_map/factors/pallas_call | solution.py:481
  6.3 30.8 %all_to_all.30.y_ref = bf16[32,8,3200]{2,1,0:T(8,128)(2,1)S(1)} all-to-all(bf16[32,8,3200]{2,1,0:T(8,128)(2,1)S(1)} %factors.1), channel_id=1, replica_groups=mesh['samp'=4,'row'=4,'col'=8] {'row','col'}, dimensions={0} | all-to-all | bytes 3276800 | tf_op jit(solution)/shard_map/all_to_all | solution.py:491
  37.0 3.9 %product.1 = (bf16[4,320,512]{2,1,0:T(8,128)(2,1)}, bf16[4,320,512]{2,1,0:T(8,128)(2,1)}, bf16[32,4,3200]{2,1,0:T(4,128)(2,1)}) custom-call(bf16[32,8,3200]{2,1,0:T(8,128)(2,1)S(1)} %all_to_all.30.y_ref), custom_call_target="tpu_custom_call" | custom-call | tf_op jit(solution)/shard_map/product/pallas_call | solution.py:432
  41.0 5.4 %all-to-all-start.1 = ((bf16[32,4,3200]{2,1,0:T(4,128)(2,1)}), bf16[32,4,3200]{2,1,0:T(4,128)(2,1)S(1)}, u32[]{:S(2)}, u32[]{:S(2)}) async-start(bf16[32,4,3200]{2,1,0:T(4,128)(2,1)} %get-tuple-element.27), calls=%async_computation.1 | async-start | bytes 1638400 | tf_op jit(solution)/shard_map/all_to_all | solution.py:507
  46.4 7.4 %gate.1 = (bf16[144,3200]{1,0:T(8,128)(2,1)}, bf16[128,3200]{1,0:T(8,128)(2,1)}, f32[128,3200]{1,0:T(8,128)}, bf16[256,3200]{1,0:T(8,128)(2,1)}, bf16[256,3200]{1,0:T(8,128)(2,1)}) custom-call(s32[1]{0:T(128)S(6)} %copy.18.crop_ref, f32[80,40,128]{2,1,0:T(8,128)} %bitcast.12, f32[80,40,128]{2,1,0:T(8,128)} %bitcast.25, f32[1,128]{1,0:T(1,128)} %bitcast.16, ...), custom_call_target="tpu_custom_call" | custom-call | flops 1000000000 | bytes 8000000 | tf_op jit(solution)/shard_map/gate/pallas_call | solution.py:492
  53.8 6.0 %all-to-all-done.1.z_ref = bf16[32,4,3200]{2,1,0:T(4,128)(2,1)S(1)} async-done(((bf16[32,4,3200]{2,1,0:T(4,128)(2,1)}), bf16[32,4,3200]{2,1,0:T(4,128)(2,1)S(1)}, u32[]{:S(2)}, u32[]{:S(2)}) %all-to-all-start.1) | async-done | bytes 819232 | tf_op jit(solution)/shard_map/all_to_all | solution.py:507
  59.8 0.0 copy-start
  59.8 0.0 copy-start.1
  59.8 4.2 %middle.1 = bf16[32,4,3200]{2,1,0:T(4,128)(2,1)S(1)} custom-call(bf16[32,4,3200]{2,1,0:T(4,128)(2,1)S(1)} %all-to-all-done.1.z_ref, bf16[128,3200]{1,0:T(8,128)(2,1)} %get-tuple-element.28.do_ref, f32[1,128]{1,0:T(1,128)} %bitcast.22, bf16[128,128]{1,0:T(8,128)(2,1)} %ow_ref.3), custom_call_target="tpu_custom_call" | custom-call | tf_op jit(solution)/shard_map/middle/pallas_call | solution.py:508
  64.0 18.6 %all_to_all.31.dp_ref = bf16[32,4,3200]{2,1,0:T(4,128)(2,1)S(1)} all-to-all(bf16[32,4,3200]{2,1,0:T(4,128)(2,1)S(1)} %middle.1), channel_id=1, replica_groups=mesh['samp'=4,'row'=4,'col'=8] {'row','col'}, dimensions={0} | all-to-all | bytes 1638400 | tf_op jit(solution)/shard_map/all_to_all | solution.py:518
  82.6 0.0 copy-done
  82.6 0.0 copy-done.1
  82.6 4.5 %slopes.1 = bf16[32,8,3200]{2,1,0:T(8,128)(2,1)} custom-call(bf16[32,4,3200]{2,1,0:T(4,128)(2,1)S(1)} %all_to_all.31.dp_ref, bf16[4,320,512]{2,1,0:T(8,128)(2,1)S(1)} %copy-done, bf16[4,320,512]{2,1,0:T(8,128)(2,1)S(1)} %copy-done.1), custom_call_target="tpu_custom_call" | custom-call | tf_op jit(solution)/shard_map/slopes/pallas_call | solution.py:447
  87.1 5.6 %all-to-all-start.3 = ((bf16[32,8,3200]{2,1,0:T(8,128)(2,1)}), bf16[32,8,3200]{2,1,0:T(8,128)(2,1)S(1)}, u32[]{:S(2)}, u32[]{:S(2)}) async-start(bf16[32,8,3200]{2,1,0:T(8,128)(2,1)} %slopes.1), calls=%async_computation.3 | async-start | bytes 3276800 | tf_op jit(solution)/shard_map/all_to_all | solution.py:533
  92.7 6.1 %outputs.1 = (bf16[128,3200]{1,0:T(8,128)(2,1)}, f32[128,128]{1,0:T(8,128)}, f32[2,128,128]{2,1,0:T(8,128)}, f32[144,128]{1,0:T(8,128)}) custom-call(bf16[32,4,3200]{2,1,0:T(4,128)(2,1)S(1)} %all-to-all-done.1.z_ref, bf16[144,3200]{1,0:T(8,128)(2,1)} %get-tuple-element.33.n_ref, bf16[128,3200]{1,0:T(8,128)(2,1)} %get-tuple-element.28.do_ref, ...), custom_call_target="tpu_custom_call" | custom-call | flops 1000000000 | bytes 8000000 | tf_op jit(solution)/shard_map/outputs/pallas_call | solution.py:519
  98.8 16.0 %all-to-all-done.3.a_ref = bf16[32,8,3200]{2,1,0:T(8,128)(2,1)S(1)} async-done(((bf16[32,8,3200]{2,1,0:T(8,128)(2,1)}), bf16[32,8,3200]{2,1,0:T(8,128)(2,1)S(1)}, u32[]{:S(2)}, u32[]{:S(2)}) %all-to-all-start.3) | async-done | bytes 1638432 | tf_op jit(solution)/shard_map/all_to_all | solution.py:533
  114.9 5.2 %weights.1 = bf16[128,8,128]{2,1,0:T(8,128)(2,1)S(1)} custom-call(bf16[32,8,3200]{2,1,0:T(8,128)(2,1)S(1)} %all-to-all-done.3.a_ref, bf16[256,3200]{1,0:T(8,128)(2,1)} %get-tuple-element.31.sv_ref, bf16[256,3200]{1,0:T(8,128)(2,1)} %get-tuple-element.32.sg_ref, bf16[144,3200]{1,0:T(8,128)(2,1)} %get-tuple-element.33.n_ref, f32[1,128]{1,0:T(1,128)} %bitcast.17, ...), custom_call_target="tpu_custom_call" | custom-call | tf_op jit(solution)/shard_map/weights/pallas_call | solution.py:534
  120.1 19.2 %all_to_all.32.x_ref = bf16[128,8,128]{2,1,0:T(8,128)(2,1)S(1)} all-to-all(bf16[128,8,128]{2,1,0:T(8,128)(2,1)S(1)} %weights.1), channel_id=1, replica_groups=mesh['samp'=4,'row'=4,'col'=8] {'samp','row','col'}, dimensions={0} | all-to-all | bytes 524288 | tf_op jit(solution)/shard_map/all_to_all | solution.py:548
  139.3 0.9 total.1
  140.2 4.4 %all-to-all-start.5 = ((bf16[128,8,128]{2,1,0:T(8,128)(2,1)}), bf16[128,8,128]{2,1,0:T(8,128)(2,1)S(1)}, u32[]{:S(2)}, u32[]{:S(2)}) async-start(bf16[128,8,128]{2,1,0:T(8,128)(2,1)} %total.1), calls=%async_computation.5 | async-start | bytes 524288 | tf_op jit(solution)/shard_map/all_to_all | solution.py:563
  144.5 6.7 %inputs.1 = f32[80,40,128]{2,1,0:T(8,128)} custom-call(f32[80,40,128]{2,1,0:T(8,128)} %bitcast.13, bf16[32,8,3200]{2,1,0:T(8,128)(2,1)S(1)} %all-to-all-done.3.a_ref, bf16[256,3200]{1,0:T(8,128)(2,1)} %get-tuple-element.31.sv_ref, bf16[256,3200]{1,0:T(8,128)(2,1)} %get-tuple-element.32.sg_ref, bf16[128,3200]{1,0:T(8,128)(2,1)} %get-tuple-element.35.dg_ref, ...), custom_call_target="tpu_custom_call" | custom-call | flops 1000000000 | bytes 8000000 | tf_op jit(solution)/shard_map/inputs/pallas_call | solution.py:549
  151.2 4.4 %all-to-all-done.5.x_ref = bf16[128,8,128]{2,1,0:T(8,128)(2,1)S(1)} async-done(((bf16[128,8,128]{2,1,0:T(8,128)(2,1)}), bf16[128,8,128]{2,1,0:T(8,128)(2,1)S(1)}, u32[]{:S(2)}, u32[]{:S(2)}) %all-to-all-start.5) | async-done | bytes 262176 | tf_op jit(solution)/shard_map/all_to_all | solution.py:563
  155.6 0.9 unpack.1
Async XLA Ops:
  41.0 18.8 %all-to-all-start.1 = ((bf16[32,4,3200]{2,1,0:T(4,128)(2,1)}), bf16[32,4,3200]{2,1,0:T(4,128)(2,1)S(1)}, u32[]{:S(2)}, u32[]{:S(2)}) async-start(bf16[32,4,3200]{2,1,0:T(4,128)(2,1)} %get-tuple-element.27), calls=%async_computation.1 | async-start | bytes 1638400 | tf_op jit(solution)/shard_map/all_to_all | solution.py:507
  59.8 22.8 %copy-start = (bf16[4,320,512]{2,1,0:T(8,128)(2,1)S(1)}, bf16[4,320,512]{2,1,0:T(8,128)(2,1)}, u32[]{:S(2)}) copy-start(bf16[4,320,512]{2,1,0:T(8,128)(2,1)} %get-tuple-element.29.l_ref) | copy-start | bytes 3932164
  59.8 22.8 %copy-start.1 = (bf16[4,320,512]{2,1,0:T(8,128)(2,1)S(1)}, bf16[4,320,512]{2,1,0:T(8,128)(2,1)}, u32[]{:S(2)}) copy-start(bf16[4,320,512]{2,1,0:T(8,128)(2,1)} %get-tuple-element.30.r_ref) | copy-start | bytes 3932164
  87.1 27.7 %all-to-all-start.3 = ((bf16[32,8,3200]{2,1,0:T(8,128)(2,1)}), bf16[32,8,3200]{2,1,0:T(8,128)(2,1)S(1)}, u32[]{:S(2)}, u32[]{:S(2)}) async-start(bf16[32,8,3200]{2,1,0:T(8,128)(2,1)} %slopes.1), calls=%async_computation.3 | async-start | bytes 3276800 | tf_op jit(solution)/shard_map/all_to_all | solution.py:533
  140.2 15.4 %all-to-all-start.5 = ((bf16[128,8,128]{2,1,0:T(8,128)(2,1)}), bf16[128,8,128]{2,1,0:T(8,128)(2,1)S(1)}, u32[]{:S(2)}, u32[]{:S(2)}) async-start(bf16[128,8,128]{2,1,0:T(8,128)(2,1)} %total.1), calls=%async_computation.5 | async-start | bytes 524288 | tf_op jit(solution)/shard_map/all_to_all | solution.py:563

commit v3 on v2

--- a/solution.py
+++ b/solution.py
@@ -122,36 +122,29 @@
     return gates, values
 
 
-def gathered(gather, buf, ref, sem):
-    part = PEERS // 4
-    copies = []
-    for q in range(4):
-        lax.fori_loop(q * part, (q + 1) * part, gather, 0, unroll=8)
-        if q:
-            copies[-1].start()
-        rows = pl.ds(q * part, part)
-        copies.append(pltpu.make_async_copy(buf.at[rows], ref.at[rows], sem.at[q]))
-    copies[-1].start()
-    return copies
-
-
-def k1(crop_ref, pair_ref, ig_ref, ib_ref, w_ref, f_ref, wg_s, wv_s, v_s):
+def k1(crop_ref, pair_ref, ig_ref, ib_ref, w_ref, f_ref, w_s, v_s):
     g = pl.program_id(0)
 
     @pl.when(g == 0)
     def _():
         perm = interleave()
         gates, values = sides(w_ref[...])
-        wg_s[...] = mm(perm, gates, 1, 1).astype(bf16)
-        wv_s[...] = mm(perm, values, 1, 1).astype(bf16)
+        w_s[: 2 * CH, :] = (0.5 * mm(perm, gates, 1, 1)).astype(bf16)
+        w_s[2 * CH :, :] = (0.5 * mm(perm, values, 1, 1)).astype(bf16)
         v_s[0] = column(ig_ref[...])
         v_s[1] = column(ib_ref[...])
 
-    hat, _ = hat_of(turned(pair_ref))
-    normed = (hat * wide(v_s[0]) + wide(v_s[1])).astype(bf16)
-    value = mm(wv_s[...], normed, 1, 0) * live_cells(crop_ref, g)
-    factor = sigmoid(mm(wg_s[...], normed, 1, 0)) * value
-    f_ref[...] = factor.astype(bf16).reshape(PEERS, 2 * OWN, STEP)
+    x = turned(pair_ref)
+    live = live_cells(crop_ref, g)
+    for lo in range(0, STEP, 256):
+        hi = min(lo + 256, STEP)
+        reps = (hi - lo) // CH
+        gain, bias = (jnp.concatenate([v_s[n]] * reps, axis=1) for n in range(2))
+        hat, _ = hat_of(x[:, lo:hi])
+        normed = (hat * gain + bias).astype(bf16)
+        both = mm(w_s[...], normed, 1, 0)
+        factor = (jnp.tanh(both[: 2 * CH]) + 1.0) * (both[2 * CH :] * live[:, lo:hi])
+        f_ref[:, :, lo:hi] = factor.astype(bf16).reshape(PEERS, 2 * OWN, hi - lo)
 
 
 def k1b(
@@ -184,7 +177,7 @@
     e_ref[...] = up * (1.0 - gate)
 
 
-def k2(y_ref, l_ref, r_ref, z_ref, x_s, p_s, l_s, r_s, z_s, sem, z_sem):
+def k2(y_ref, _, l_ref, r_ref, z_ref, x_s, p_s, l_s, r_s, sem):
     def spread(s, carry):
         r, c = peers_of(s)
         rows = y_ref[s].astype(f32)
@@ -218,10 +211,11 @@
         first = (c >> 1) * 128 + (c & 1) * WIDE
         for g in range(STEPS):
             pieces = [p_s[r, pl.ds(first + g * 8 + k, OWN, stride=JPITCH), :] for k in range(8)]
-            z_s[s, :, g * STEP : (g + 1) * STEP] = fold(pieces).astype(bf16)
+            z_ref[s, :, g * STEP : (g + 1) * STEP] = fold(pieces).astype(bf16)
         return carry
 
-    for copy in copies + gathered(gather, z_s, z_ref, z_sem):
+    lax.fori_loop(0, PEERS, gather, 0, unroll=8)
+    for copy in copies:
         copy.wait()
 
 
@@ -268,7 +262,10 @@
     gv_ref[1] += lane_fold(up)
 
 
-def k4(dp_ref, l_ref, r_ref, a_ref, x_s, o_s, a_s, sem):
+def k4(dp_ref, l_ref, r_ref, _, a_ref, x_s, o_s, l_s, r_s, sem):
+    copies = [pltpu.make_async_copy(l_ref, l_s, sem.at[0]), pltpu.make_async_copy(r_ref, r_s, sem.at[1])]
+    for copy in copies:
+        copy.start()
     zero = jnp.zeros((128 - TALL, 128), f32)
     for r in range(ROWS):
         for h in range(OWN):
@@ -285,7 +282,9 @@
                 x_s[r, pl.ds(first + g * 8 + k, OWN, stride=JPITCH), :] = v
         return carry
 
-    lax.fori_loop(0, PEERS, spread, 0, unroll=8)
+    lax.fori_loop(0, PEERS, spread, 0, unroll=16)
+    for copy in copies:
+        copy.wait()
     lane = lax.broadcasted_iota(jnp.int32, (ROWS * 128, 128), 1)
     for h in range(OWN):
         parts = []
@@ -293,8 +292,8 @@
             x = x_s[r, h * JPITCH : h * JPITCH + ROWS * 128, :]
             parts.append(jnp.where(lane < TALL, x, 0.0).astype(bf16))
         dp = jnp.concatenate(parts, axis=1)
-        d_left = mm(r_ref[h], dp, 1, 0)
-        d_right = mm(l_ref[h], dp, 1, 1)
+        d_left = mm(r_s[h], dp, 1, 0)
+        d_right = mm(l_s[h], dp, 1, 1)
         for r in range(ROWS):
             o_s[r, h * PITCH : h * PITCH + FULL, :] = d_left[:, r * 128 : (r + 1) * 128]
             at = (OWN + h) * PITCH
@@ -304,37 +303,36 @@
         r, c = peers_of(s)
         for g in range(STEPS):
             pieces = [o_s[r, pl.ds(c * WIDE + g * 8 + k, 2 * OWN, stride=PITCH), :] for k in range(8)]
-            a_s[s, :, g * STEP : (g + 1) * STEP] = fold(pieces).astype(bf16)
+            a_ref[s, :, g * STEP : (g + 1) * STEP] = fold(pieces).astype(bf16)
         return carry
 
-    for copy in gathered(gather, a_s, a_ref, sem):
-        copy.wait()
+    lax.fori_loop(0, PEERS, gather, 0, unroll=16)
 
 
 def k5(
     a_ref, sv_ref, sg_ref, n_ref, ig_ref, ib_ref, w_ref, gw_ref, gow_ref, gv_ref, gg_ref,
-    s_ref, ag_s, av_s, pk_s,
+    s_ref, ag_s, pk_s,
 ):
     g = pl.program_id(0)
 
     @pl.when(g == 0)
     def _():
         ag_s[...] = jnp.zeros_like(ag_s)
-        av_s[...] = jnp.zeros_like(av_s)
 
     d = a_ref[...].reshape(2 * CH, STEP).astype(f32)
-    normed = n_ref[...]
-    ag_s[...] += mm(normed, (d * sg_ref[...].astype(f32)).astype(bf16), 1, 1)
-    av_s[...] += mm(normed, (d * sv_ref[...].astype(f32)).astype(bf16), 1, 1)
+    d_gates = (d * sg_ref[...].astype(f32)).astype(bf16)
+    d_values = (d * sv_ref[...].astype(f32)).astype(bf16)
+    ag_s[...] += mm(jnp.concatenate([d_gates, d_values], axis=0), n_ref[...], 1, 1)
 
     @pl.when(g == STEPS - 1)
     def _():
         perm = interleave()
         gates, values = sides(w_ref[...])
+        g_gates, g_values = ag_s[: 2 * CH, :].T, ag_s[2 * CH :, :].T
         weights = (mm(gates, perm, 1, 1), mm(values, perm, 1, 1), gw_ref[...].astype(f32))
         slope = jnp.zeros((CH, 1), f32)
         shift = jnp.zeros((CH, 1), f32)
-        for weight, grad in zip(weights, (ag_s, av_s, gg_ref)):
+        for weight, grad in zip(weights, (g_gates, g_values, gg_ref[...])):
             slope += jnp.sum(weight * grad[:CH, :], axis=1, keepdims=True)
             shift += jnp.sum(weight * grad[CH : CH + 1, :], axis=1, keepdims=True)
         gain, bias = column(ig_ref[...]), column(ib_ref[...])
@@ -342,8 +340,8 @@
         sums = jnp.where(lane == 0, (slope - bias * shift) / gain, jnp.where(lane == 1, shift, 0.0))
         for n in range(2):
             sums = jnp.where(lane == 2 + n, jnp.sum(gv_ref[n], axis=1, keepdims=True), sums)
-        d_gates = mm(ag_s[:CH, :].astype(bf16), perm, 1, 0)
-        d_values = mm(av_s[:CH, :].astype(bf16), perm, 1, 0)
+        d_gates = mm(g_gates[:CH, :].astype(bf16), perm, 1, 0)
+        d_values = mm(g_values[:CH, :].astype(bf16), perm, 1, 0)
         planes = (
             d_gates[:, :CH], d_values[:, :CH], d_gates[:, CH:], d_values[:, CH:],
             gg_ref[:CH, :], gow_ref[...], sums, jnp.zeros((CH, CH), f32),
@@ -428,33 +426,39 @@
     return pltpu.VMEM(shape, dtype)
 
 
-def product_call(factors, name):
+HERE = pl.BlockSpec(memory_space=pltpu.VMEM)
+AWAY = pl.BlockSpec(memory_space=pltpu.HBM)
+KEPT = (OWN, FULL, ROWS * 128)
+
+
+def product_call(factors, after, name):
     return pl.pallas_call(
         k2,
         name=name,
         compiler_params=LARGE,
-        out_specs=[pl.BlockSpec(memory_space=pltpu.HBM)] * 3,
-        out_shape=[away((OWN, FULL, ROWS * 128), bf16)] * 2 + [away((PEERS, OWN, CELLS), bf16)],
+        in_specs=[HERE, AWAY],
+        out_specs=[AWAY, AWAY, HERE],
+        out_shape=[away(KEPT, bf16), away(KEPT, bf16), out((PEERS, OWN, CELLS), bf16)],
         scratch_shapes=[
             vm(ROWS, 2 * OWN * PITCH, 128), vm(ROWS, OWN * JPITCH, 128),
-            vm(OWN, FULL, ROWS * 128, dtype=bf16), vm(OWN, FULL, ROWS * 128, dtype=bf16),
-            vm(PEERS, OWN, CELLS, dtype=bf16), pltpu.SemaphoreType.DMA((2,)), pltpu.SemaphoreType.DMA((4,)),
+            vm(*KEPT, dtype=bf16), vm(*KEPT, dtype=bf16), pltpu.SemaphoreType.DMA((2,)),
         ],
-    )(factors)
-
-
-def slopes_call(d_product, left, right, name):
+    )(factors, *keep_away(after))
+
+
+def slopes_call(d_product, left, right, after, name):
     return pl.pallas_call(
         k4,
         name=name,
         compiler_params=LARGE,
-        out_specs=pl.BlockSpec(memory_space=pltpu.HBM),
-        out_shape=away((PEERS, 2 * OWN, CELLS), bf16),
+        in_specs=[HERE, AWAY, AWAY, AWAY],
+        out_specs=HERE,
+        out_shape=out((PEERS, 2 * OWN, CELLS), bf16),
         scratch_shapes=[
             vm(ROWS, OWN * JPITCH, 128), vm(ROWS, 2 * OWN * PITCH, 128),
-            vm(PEERS, 2 * OWN, CELLS, dtype=bf16), pltpu.SemaphoreType.DMA((4,)),
+            vm(*KEPT, dtype=bf16), vm(*KEPT, dtype=bf16), pltpu.SemaphoreType.DMA((2,)),
         ],
-    )(d_product, left, right)
+    )(d_product, *keep_away(left, right, after))
 
 
 def per_device(
@@ -486,7 +490,7 @@
         in_specs=[SMEM, tile(), one, one, proj],
         out_specs=lanes(PEERS, 2 * OWN),
         out_shape=out(both, bf16),
-        scratch_shapes=[wb(2 * CH, CH), wb(2 * CH, CH), vm(2, CH, CH)],
+        scratch_shapes=[wb(4 * CH, CH), vm(2, CH, CH)],
     )(crop_length, *keep_away(pair, in_gain, in_bias, proj_weight))
     factors = swap(factors, group)
     normed, d_out, slope, by_value, by_gate = pl.pallas_call(
@@ -503,7 +507,7 @@
         scratch_shapes=[wb(2 * CH, CH), wb(2 * CH, CH), wb(CH, CH), vm(2, CH, CH)],
         cost_estimate=cost,
     )(crop_length, *keep_away(pair, cotangent, in_gain, in_bias, proj_weight, gate_weight))
-    left, right, product = product_call(factors, "product")
+    left, right, product = product_call(factors, d_out, "product")
     product = swap(product, group)
     d_product = pl.pallas_call(
         k3,
@@ -514,7 +518,7 @@
         out_specs=lanes(PEERS, OWN),
         out_shape=out((PEERS, OWN, CELLS), bf16),
         scratch_shapes=[vm(CH, STEP), vm(CH, CH)],
-    )(product, *keep_away(d_out, out_gain, out_weight))
+    )(product, d_out, out_gain, out_weight)
     d_product = swap(d_product, group)
     d_gate, g_out_weight, g_out, g_gate = pl.pallas_call(
         k3b,
@@ -529,7 +533,7 @@
         scratch_shapes=[vm(CH, STEP), wb(CH, CH), vm(2, CH, CH)],
         cost_estimate=cost,
     )(product, *keep_away(normed, d_out, slope, out_gain, out_bias, out_weight))
-    d_factors = slopes_call(d_product, left, right, "slopes")
+    d_factors = slopes_call(d_product, left, right, d_gate, "slopes")
     d_factors = swap(d_factors, group)
     packed = pl.pallas_call(
         k5,
@@ -542,9 +546,9 @@
         ],
         out_specs=whole(CH, 8, CH),
         out_shape=out((CH, 8, CH), bf16),
-        scratch_shapes=[vm(CH + 16, 2 * CH), vm(CH + 16, 2 * CH), vm(CH * 8, CH)],
-    )(d_factors, *keep_away(by_value, by_gate, normed, in_gain, in_bias, proj_weight, gate_weight,
-                            g_out_weight, g_out, g_gate))
+        scratch_shapes=[vm(4 * CH, CH + 16), vm(CH * 8, CH)],
+    )(d_factors, by_value, by_gate, normed, in_gain, in_bias, proj_weight, gate_weight,
+      g_out_weight, g_out, g_gate)
     parts = swap(packed, everyone)
     grad_pair = pl.pallas_call(
         k5b,

time: 157 us -> 155 us (0.987)
  starting transfers between devices: 15.3 us -> 18.4 us
  blocking collectives: 68.5 us -> 65.4 us
  Pallas kernels: 44.8 us -> 41.9 us
    all_to_all x2, starting transfers between devices: 11 us -> 14.1 us  [the longest x1 8.57 us: per_device(): factors = swap(factors, group)]
    all_to_all x2, blocking collectives: 49.4 us -> 46.3 us  [the longest x1 27.9 us: per_device(): d_factors = swap(d_factors, group)]
    pallas_call x1, Pallas kernels: 5.24 us -> 3.12 us  [per_device(): pl.pallas_call(k5, name='weights', compiler_params=SMALL, grid=(STEPS,),...]
where the time goes in v3:
time: 155 us; the launch traced here: 154 us
  blocking collectives  65.4 us (42%)
  Pallas kernels  41.9 us (27%)
  waiting for transfers between devices  26.5 us (17%)
  starting transfers between devices  18.4 us (12%)
    all_to_all x1, blocking collectives, per_device(): d_factors = swap(d_factors, group)  27.9 us
    all_to_all x1, blocking collectives, per_device(): parts = swap(packed, everyone)  19 us
    all_to_all x1, blocking collectives, per_device(): product = swap(product, group)  18.4 us
    all_to_all x1, waiting for transfers between devices, per_device(): factors = swap(factors, group)  14.8 us
    all_to_all x1, starting transfers between devices, per_device(): factors = swap(factors, group)  8.57 us
    pallas_call x1, Pallas kernels, per_device(): pl.pallas_call(k1b, name='gate', compiler_params=SMALL, grid=(STEPS,), in...  7.43 us
    all_to_all x1, waiting for transfers between devices, per_device(): d_product = swap(d_product, group)  7.25 us
    pallas_call x1, Pallas kernels, per_device(): pl.pallas_call(k5b, name='inputs', compiler_params=SMALL, grid=(STEPS,),...  6.66 us
  transfers between devices with their start and end apart: 3, of which 3 were waited for; matrix products, arithmetic and copies ran while one was open for 0% of the time, Pallas kernels for 13%

profile of v3, /device:TPU:1, one launch (start us, length us, event | category | flops | bytes accessed | tf_op | source)
XLA Modules:
  0.0 153.7 jit_solution(11655248071798032819)
XLA Ops:
  1.3 5.8 %factors.1 = bf16[32,8,3200]{2,1,0:T(8,128)(2,1)} custom-call(s32[1]{0:T(128)S(6)} %copy.18.crop_ref, f32[80,40,128]{2,1,0:T(8,128)} %bitcast.20, f32[1,128]{1,0:T(1,128)} %bitcast.11, f32[1,128]{1,0:T(1,128)} %bitcast.15, bf16[128,512]{1,0:T(8,128)(2,1)} %w_ref.7), custom_call_target="tpu_custom_call" | custom-call | tf_op jit(solution)/shard_map/factors/pallas_call | solution.py:485
  7.0 8.6 %all-to-all-start = ((bf16[32,8,3200]{2,1,0:T(8,128)(2,1)}), bf16[32,8,3200]{2,1,0:T(8,128)(2,1)S(1)}, u32[]{:S(2)}, u32[]{:S(2)}) async-start(bf16[32,8,3200]{2,1,0:T(8,128)(2,1)} %factors.1), calls=%async_computation | async-start | bytes 3276800 | tf_op jit(solution)/shard_map/all_to_all | solution.py:495
  15.6 7.4 %gate.1 = (bf16[144,3200]{1,0:T(8,128)(2,1)}, bf16[128,3200]{1,0:T(8,128)(2,1)}, f32[128,3200]{1,0:T(8,128)}, bf16[256,3200]{1,0:T(8,128)(2,1)}, bf16[256,3200]{1,0:T(8,128)(2,1)}) custom-call(s32[1]{0:T(128)S(6)} %copy.18.crop_ref, f32[80,40,128]{2,1,0:T(8,128)} %bitcast.21, f32[80,40,128]{2,1,0:T(8,128)} %bitcast.25, f32[1,128]{1,0:T(1,128)} %bitcast.12, ...), custom_call_target="tpu_custom_call" | custom-call | flops 1000000000 | bytes 8000000 | tf_op jit(solution)/shard_map/gate/pallas_call | solution.py:496
  23.0 14.8 %all-to-all-done.y_ref = bf16[32,8,3200]{2,1,0:T(8,128)(2,1)S(1)} async-done(((bf16[32,8,3200]{2,1,0:T(8,128)(2,1)}), bf16[32,8,3200]{2,1,0:T(8,128)(2,1)S(1)}, u32[]{:S(2)}, u32[]{:S(2)}) %all-to-all-start) | async-done | bytes 1638432 | tf_op jit(solution)/shard_map/all_to_all | solution.py:495
  37.8 0.0 copy-start
  37.8 0.0 copy-start.5
  37.8 0.0 copy-start.12
  37.8 3.5 %product.1 = (bf16[4,320,512]{2,1,0:T(8,128)(2,1)}, bf16[4,320,512]{2,1,0:T(8,128)(2,1)}, bf16[32,4,3200]{2,1,0:T(4,128)(2,1)S(1)}) custom-call(bf16[32,8,3200]{2,1,0:T(8,128)(2,1)S(1)} %all-to-all-done.y_ref, bf16[128,3200]{1,0:T(8,128)(2,1)} %get-tuple-element.27._.do_ref), custom_call_target="tpu_custom_call" | custom-call | tf_op jit(solution)/shard_map/product/pallas_call | solution.py:435
  41.4 18.4 %all_to_all.30.z_ref = bf16[32,4,3200]{2,1,0:T(4,128)(2,1)S(1)} all-to-all(bf16[32,4,3200]{2,1,0:T(4,128)(2,1)S(1)} %get-tuple-element.28), channel_id=1, replica_groups=mesh['samp'=4,'row'=4,'col'=8] {'row','col'}, dimensions={0} | all-to-all | bytes 1638400 | tf_op jit(solution)/shard_map/all_to_all | solution.py:511
  59.8 0.0 copy-done
  59.8 0.0 copy-done.5
  59.8 0.0 copy-done.12
  59.8 3.3 %middle.1 = bf16[32,4,3200]{2,1,0:T(4,128)(2,1)} custom-call(bf16[32,4,3200]{2,1,0:T(4,128)(2,1)S(1)} %all_to_all.30.z_ref, bf16[128,3200]{1,0:T(8,128)(2,1)S(1)} %copy-done, f32[1,128]{1,0:T(1,128)S(1)} %bitcast.19, bf16[128,128]{1,0:T(8,128)(2,1)S(1)} %copy-done.5), custom_call_target="tpu_custom_call" | custom-call | tf_op jit(solution)/shard_map/middle/pallas_call | solution.py:512
  63.2 5.5 %all-to-all-start.2 = ((bf16[32,4,3200]{2,1,0:T(4,128)(2,1)}), bf16[32,4,3200]{2,1,0:T(4,128)(2,1)S(1)}, u32[]{:S(2)}, u32[]{:S(2)}) async-start(bf16[32,4,3200]{2,1,0:T(4,128)(2,1)} %middle.1), calls=%async_computation.2 | async-start | bytes 1638400 | tf_op jit(solution)/shard_map/all_to_all | solution.py:522
  68.6 6.1 %outputs.1 = (bf16[128,3200]{1,0:T(8,128)(2,1)}, f32[128,128]{1,0:T(8,128)}, f32[2,128,128]{2,1,0:T(8,128)}, f32[144,128]{1,0:T(8,128)}) custom-call(bf16[32,4,3200]{2,1,0:T(4,128)(2,1)S(1)} %all_to_all.30.z_ref, bf16[144,3200]{1,0:T(8,128)(2,1)} %get-tuple-element.31.n_ref, bf16[128,3200]{1,0:T(8,128)(2,1)} %get-tuple-element.27._.do_ref, ...), custom_call_target="tpu_custom_call" | custom-call | flops 1000000000 | bytes 8000000 | tf_op jit(solution)/shard_map/outputs/pallas_call | solution.py:523
  74.8 7.3 %all-to-all-done.2.dp_ref = bf16[32,4,3200]{2,1,0:T(4,128)(2,1)S(1)} async-done(((bf16[32,4,3200]{2,1,0:T(4,128)(2,1)}), bf16[32,4,3200]{2,1,0:T(4,128)(2,1)S(1)}, u32[]{:S(2)}, u32[]{:S(2)}) %all-to-all-start.2) | async-done | bytes 819232 | tf_op jit(solution)/shard_map/all_to_all | solution.py:522
  82.0 0.0 copy-start.3
  82.0 0.0 copy-start.4
  82.0 0.0 copy-start.6
  82.0 0.0 copy-start.7
  82.0 0.0 copy-start.8
  82.0 0.0 copy-start.9
  82.1 4.2 %slopes.1 = bf16[32,8,3200]{2,1,0:T(8,128)(2,1)S(1)} custom-call(bf16[32,4,3200]{2,1,0:T(4,128)(2,1)S(1)} %all-to-all-done.2.dp_ref, bf16[4,320,512]{2,1,0:T(8,128)(2,1)} %get-tuple-element.29.l_ref, bf16[4,320,512]{2,1,0:T(8,128)(2,1)} %get-tuple-element.30.r_ref, bf16[128,3200]{1,0:T(8,128)(2,1)} %get-tuple-element.33._.dg_ref), custom_call_target="tpu_custom_call" | custom-call | tf_op jit(solution)/shard_map/slopes/pallas_call | solution.py:450
  86.3 0.0 copy-start.1
  86.3 0.0 copy-start.2
  86.3 0.0 copy-start.10
  86.3 0.0 copy-start.11
  86.3 27.9 %all_to_all.31.a_ref = bf16[32,8,3200]{2,1,0:T(8,128)(2,1)S(1)} all-to-all(bf16[32,8,3200]{2,1,0:T(8,128)(2,1)S(1)} %slopes.1), channel_id=1, replica_groups=mesh['samp'=4,'row'=4,'col'=8] {'row','col'}, dimensions={0} | all-to-all | bytes 3276800 | tf_op jit(solution)/shard_map/all_to_all | solution.py:537
  114.2 0.0 copy-done.3
  114.2 0.0 copy-done.4
  114.2 0.0 copy-done.6
  114.3 0.0 copy-done.7
  114.3 0.0 copy-done.8
  114.3 0.0 copy-done.9
  114.3 0.0 copy-done.1
  114.3 0.0 copy-done.2
  114.3 0.0 copy-done.10
  114.3 0.0 copy-done.11
  114.3 3.1 %weights.1 = bf16[128,8,128]{2,1,0:T(8,128)(2,1)S(1)} custom-call(bf16[32,8,3200]{2,1,0:T(8,128)(2,1)S(1)} %all_to_all.31.a_ref, bf16[256,3200]{1,0:T(8,128)(2,1)S(1)} %copy-done.1, bf16[256,3200]{1,0:T(8,128)(2,1)S(1)} %copy-done.2, bf16[144,3200]{1,0:T(8,128)(2,1)S(1)} %copy-done.3, f32[1,128]{1,0:T(1,128)S(1)} %bitcast.14, f32[1,128]{1,0:T(1,128)S(1)} %bitcast.17, ...), custom_call_target="tpu_custom_call" | custom-call | tf_op jit(solution)/shard_map/weights/pallas_call | solution.py:538
  117.4 19.0 %all_to_all.32.x_ref = bf16[128,8,128]{2,1,0:T(8,128)(2,1)S(1)} all-to-all(bf16[128,8,128]{2,1,0:T(8,128)(2,1)S(1)} %weights.1), channel_id=1, replica_groups=mesh['samp'=4,'row'=4,'col'=8] {'samp','row','col'}, dimensions={0} | all-to-all | bytes 524288 | tf_op jit(solution)/shard_map/all_to_all | solution.py:552
  136.5 0.9 total.1
  137.3 4.4 %all-to-all-start.5 = ((bf16[128,8,128]{2,1,0:T(8,128)(2,1)}), bf16[128,8,128]{2,1,0:T(8,128)(2,1)S(1)}, u32[]{:S(2)}, u32[]{:S(2)}) async-start(bf16[128,8,128]{2,1,0:T(8,128)(2,1)} %total.1), calls=%async_computation.5 | async-start | bytes 524288 | tf_op jit(solution)/shard_map/all_to_all | solution.py:567
  141.7 6.7 %inputs.1 = f32[80,40,128]{2,1,0:T(8,128)} custom-call(f32[80,40,128]{2,1,0:T(8,128)} %bitcast.22, bf16[32,8,3200]{2,1,0:T(8,128)(2,1)S(1)} %all_to_all.31.a_ref, bf16[256,3200]{1,0:T(8,128)(2,1)} %get-tuple-element.34.sv_ref, bf16[256,3200]{1,0:T(8,128)(2,1)} %get-tuple-element.35.sg_ref, bf16[128,3200]{1,0:T(8,128)(2,1)} %get-tuple-element.33._.dg_ref, ...), custom_call_target="tpu_custom_call" | custom-call | flops 1000000000 | bytes 8000000 | tf_op jit(solution)/shard_map/inputs/pallas_call | solution.py:553
  148.4 4.4 %all-to-all-done.5.x_ref = bf16[128,8,128]{2,1,0:T(8,128)(2,1)S(1)} async-done(((bf16[128,8,128]{2,1,0:T(8,128)(2,1)}), bf16[128,8,128]{2,1,0:T(8,128)(2,1)S(1)}, u32[]{:S(2)}, u32[]{:S(2)}) %all-to-all-start.5) | async-done | bytes 262176 | tf_op jit(solution)/shard_map/all_to_all | solution.py:567
  152.8 0.9 unpack.1
Async XLA Ops:
  7.0 30.8 %all-to-all-start = ((bf16[32,8,3200]{2,1,0:T(8,128)(2,1)}), bf16[32,8,3200]{2,1,0:T(8,128)(2,1)S(1)}, u32[]{:S(2)}, u32[]{:S(2)}) async-start(bf16[32,8,3200]{2,1,0:T(8,128)(2,1)} %factors.1), calls=%async_computation | async-start | bytes 3276800 | tf_op jit(solution)/shard_map/all_to_all | solution.py:495
  37.8 22.0 %copy-start = (bf16[128,3200]{1,0:T(8,128)(2,1)S(1)}, bf16[128,3200]{1,0:T(8,128)(2,1)}, u32[]{:S(2)}) copy-start(bf16[128,3200]{1,0:T(8,128)(2,1)} %get-tuple-element.27._.do_ref) | copy-start | bytes 2457604
  37.8 22.0 %copy-start.5 = (bf16[128,128]{1,0:T(8,128)(2,1)S(1)}, bf16[128,128]{1,0:T(8,128)(2,1)}, u32[]{:S(2)}) copy-start(bf16[128,128]{1,0:T(8,128)(2,1)} %ow_ref.3) | copy-start | bytes 98308
  37.8 22.0 %copy-start.12 = (f32[128]{0:T(128)S(1)}, f32[128]{0:T(128)}, u32[]{:S(2)}) copy-start(f32[128]{0:T(128)} %param.17) | copy-start | bytes 1540
  63.2 18.9 %all-to-all-start.2 = ((bf16[32,4,3200]{2,1,0:T(4,128)(2,1)}), bf16[32,4,3200]{2,1,0:T(4,128)(2,1)S(1)}, u32[]{:S(2)}, u32[]{:S(2)}) async-start(bf16[32,4,3200]{2,1,0:T(4,128)(2,1)} %middle.1), calls=%async_computation.2 | async-start | bytes 1638400 | tf_op jit(solution)/shard_map/all_to_all | solution.py:522
  82.0 32.2 %copy-start.3 = (bf16[144,3200]{1,0:T(8,128)(2,1)S(1)}, bf16[144,3200]{1,0:T(8,128)(2,1)}, u32[]{:S(2)}) copy-start(bf16[144,3200]{1,0:T(8,128)(2,1)} %get-tuple-element.31.n_ref) | copy-start | bytes 2764804
  82.0 32.2 %copy-start.4 = (bf16[128,512]{1,0:T(8,128)(2,1)S(1)}, bf16[128,512]{1,0:T(8,128)(2,1)}, u32[]{:S(2)}) copy-start(bf16[128,512]{1,0:T(8,128)(2,1)} %w_ref.7) | copy-start | bytes 393220
  82.0 32.2 %copy-start.6 = (bf16[128,128]{1,0:T(8,128)(2,1)S(1)}, bf16[128,128]{1,0:T(8,128)(2,1)}, u32[]{:S(2)}) copy-start(bf16[128,128]{1,0:T(8,128)(2,1)} %gw_ref.5) | copy-start | bytes 98308
  82.0 32.2 %copy-start.7 = (f32[2,128,128]{2,1,0:T(8,128)S(1)}, f32[2,128,128]{2,1,0:T(8,128)}, u32[]{:S(2)}) copy-start(f32[2,128,128]{2,1,0:T(8,128)} %get-tuple-element.37.gv_ref) | copy-start | bytes 393220
  82.0 32.2 %copy-start.8 = (f32[144,128]{1,0:T(8,128)S(1)}, f32[144,128]{1,0:T(8,128)}, u32[]{:S(2)}) copy-start(f32[144,128]{1,0:T(8,128)} %get-tuple-element.38.gg_ref) | copy-start | bytes 221188
  82.0 32.2 %copy-start.9 = (f32[128,128]{1,0:T(8,128)S(1)}, f32[128,128]{1,0:T(8,128)}, u32[]{:S(2)}) copy-start(f32[128,128]{1,0:T(8,128)} %get-tuple-element.36.gow_ref) | copy-start | bytes 196612
  86.3 28.0 %copy-start.1 = (bf16[256,3200]{1,0:T(8,128)(2,1)S(1)}, bf16[256,3200]{1,0:T(8,128)(2,1)}, u32[]{:S(2)}) copy-start(bf16[256,3200]{1,0:T(8,128)(2,1)} %get-tuple-element.34.sv_ref) | copy-start | bytes 4915204
  86.3 28.0 %copy-start.2 = (bf16[256,3200]{1,0:T(8,128)(2,1)S(1)}, bf16[256,3200]{1,0:T(8,128)(2,1)}, u32[]{:S(2)}) copy-start(bf16[256,3200]{1,0:T(8,128)(2,1)} %get-tuple-element.35.sg_ref) | copy-start | bytes 4915204
  86.3 28.0 %copy-start.10 = (f32[128]{0:T(128)S(1)}, f32[128]{0:T(128)}, u32[]{:S(2)}) copy-start(f32[128]{0:T(128)} %param.13) | copy-start | bytes 1540
  86.3 28.0 %copy-start.11 = (f32[128]{0:T(128)S(1)}, f32[128]{0:T(128)}, u32[]{:S(2)}) copy-start(f32[128]{0:T(128)} %param.14) | copy-start | bytes 1540
  137.3 15.4 %all-to-all-start.5 = ((bf16[128,8,128]{2,1,0:T(8,128)(2,1)}), bf16[128,8,128]{2,1,0:T(8,128)(2,1)S(1)}, u32[]{:S(2)}, u32[]{:S(2)}) async-start(bf16[128,8,128]{2,1,0:T(8,128)(2,1)} %total.1), calls=%async_computation.5 | async-start | bytes 524288 | tf_op jit(solution)/shard_map/all_to_all | solution.py:567

commit v4 on v3

--- a/solution.py
+++ b/solution.py
@@ -195,10 +195,10 @@
 
     for h in range(OWN):
         left = matrix(h).astype(bf16)
-        right = matrix(OWN + h)
+        right = matrix(OWN + h).astype(bf16)
         l_s[h] = left
-        r_s[h] = right.astype(bf16)
-        product = mm(right.T.astype(bf16), left, 1, 0)
+        r_s[h] = right
+        product = mm(right, left, 0, 0)
         for r in range(ROWS):
             p_s[r, h * JPITCH : h * JPITCH + ROWS * 128, :] = product[:, r * 128 : (r + 1) * 128]
 
@@ -219,20 +219,26 @@
         copy.wait()
 
 
-def k3(z_ref, do_ref, og_ref, ow_ref, dp_ref, z_s, v_s):
-    @pl.when(pl.program_id(0) == 0)
-    def _():
-        v_s[...] = column(og_ref[...])
-
-    for d in range(PEERS):
-        z_s[d * OWN : (d + 1) * OWN, :] = z_ref[d].astype(f32)
-    hat, inverse = hat_of(z_s[...])
-    scaled = mm(ow_ref[...], do_ref[...], 1, 0) * wide(v_s[...])
-    m1 = jnp.mean(scaled, axis=0, keepdims=True)
-    m2 = jnp.mean(scaled * hat, axis=0, keepdims=True)
-    z_s[...] = inverse * (scaled - m1 - hat * m2)
-    for d in range(PEERS):
-        dp_ref[d] = z_s[d * OWN : (d + 1) * OWN, :].astype(bf16)
+def k3(z_ref, do_ref, og_ref, ow_ref, dp_ref, z_s, b_s, sem):
+    gain = wide(column(og_ref[...]))
+    copies = []
+    for g in range(STEPS):
+        at = pl.ds(g * STEP, STEP)
+        for d in range(PEERS):
+            z_s[g, d * OWN : (d + 1) * OWN, :] = z_ref[d, :, at].astype(f32)
+        hat, inverse = hat_of(z_s[g])
+        scaled = mm(ow_ref[...], do_ref[:, at], 1, 0) * gain
+        m1 = jnp.mean(scaled, axis=0, keepdims=True)
+        m2 = jnp.mean(scaled * hat, axis=0, keepdims=True)
+        z_s[g] = inverse * (scaled - m1 - hat * m2)
+        for d in range(PEERS):
+            b_s[d, :, at] = z_s[g, d * OWN : (d + 1) * OWN, :].astype(bf16)
+        if copies:
+            copies[-1].start()
+        copies.append(pltpu.make_async_copy(b_s.at[:, :, at], dp_ref.at[:, :, at], sem.at[g]))
+    copies[-1].start()
+    for copy in copies:
+        copy.wait()
 
 
 def k3b(
@@ -313,42 +319,37 @@
     a_ref, sv_ref, sg_ref, n_ref, ig_ref, ib_ref, w_ref, gw_ref, gow_ref, gv_ref, gg_ref,
     s_ref, ag_s, pk_s,
 ):
-    g = pl.program_id(0)
-
-    @pl.when(g == 0)
-    def _():
-        ag_s[...] = jnp.zeros_like(ag_s)
-
-    d = a_ref[...].reshape(2 * CH, STEP).astype(f32)
-    d_gates = (d * sg_ref[...].astype(f32)).astype(bf16)
-    d_values = (d * sv_ref[...].astype(f32)).astype(bf16)
-    ag_s[...] += mm(jnp.concatenate([d_gates, d_values], axis=0), n_ref[...], 1, 1)
-
-    @pl.when(g == STEPS - 1)
-    def _():
-        perm = interleave()
-        gates, values = sides(w_ref[...])
-        g_gates, g_values = ag_s[: 2 * CH, :].T, ag_s[2 * CH :, :].T
-        weights = (mm(gates, perm, 1, 1), mm(values, perm, 1, 1), gw_ref[...].astype(f32))
-        slope = jnp.zeros((CH, 1), f32)
-        shift = jnp.zeros((CH, 1), f32)
-        for weight, grad in zip(weights, (g_gates, g_values, gg_ref[...])):
-            slope += jnp.sum(weight * grad[:CH, :], axis=1, keepdims=True)
-            shift += jnp.sum(weight * grad[CH : CH + 1, :], axis=1, keepdims=True)
-        gain, bias = column(ig_ref[...]), column(ib_ref[...])
-        lane = lax.broadcasted_iota(jnp.int32, (CH, CH), 1)
-        sums = jnp.where(lane == 0, (slope - bias * shift) / gain, jnp.where(lane == 1, shift, 0.0))
-        for n in range(2):
-            sums = jnp.where(lane == 2 + n, jnp.sum(gv_ref[n], axis=1, keepdims=True), sums)
-        d_gates = mm(g_gates[:CH, :].astype(bf16), perm, 1, 0)
-        d_values = mm(g_values[:CH, :].astype(bf16), perm, 1, 0)
-        planes = (
-            d_gates[:, :CH], d_values[:, :CH], d_gates[:, CH:], d_values[:, CH:],
-            gg_ref[:CH, :], gow_ref[...], sums, jnp.zeros((CH, CH), f32),
-        )
-        for n, plane in enumerate(planes):
-            pk_s[pl.ds(n, CH, stride=8), :] = plane
-        s_ref[...] = pk_s[...].astype(bf16).reshape(CH, 8, CH)
+    total = None
+    for g in range(STEPS):
+        at = slice(g * STEP, (g + 1) * STEP)
+        d = a_ref[:, :, at].reshape(2 * CH, STEP)
+        slopes = jnp.concatenate([d * sg_ref[:, at], d * sv_ref[:, at]], axis=0)
+        part = mm(slopes, n_ref[:, at], 1, 1)
+        total = part if total is None else total + part
+    ag_s[...] = total
+    perm = interleave()
+    gates, values = sides(w_ref[...])
+    g_gates, g_values = ag_s[: 2 * CH, :].T, ag_s[2 * CH :, :].T
+    weights = (mm(gates, perm, 1, 1), mm(values, perm, 1, 1), gw_ref[...].astype(f32))
+    slope = jnp.zeros((CH, 1), f32)
+    shift = jnp.zeros((CH, 1), f32)
+    for weight, grad in zip(weights, (g_gates, g_values, gg_ref[...])):
+        slope += jnp.sum(weight * grad[:CH, :], axis=1, keepdims=True)
+        shift += jnp.sum(weight * grad[CH : CH + 1, :], axis=1, keepdims=True)
+    gain, bias = column(ig_ref[...]), column(ib_ref[...])
+    lane = lax.broadcasted_iota(jnp.int32, (CH, CH), 1)
+    sums = jnp.where(lane == 0, (slope - bias * shift) / gain, jnp.where(lane == 1, shift, 0.0))
+    for n in range(2):
+        sums = jnp.where(lane == 2 + n, jnp.sum(gv_ref[n], axis=1, keepdims=True), sums)
+    d_gates = mm(g_gates[:CH, :].astype(bf16), perm, 1, 0)
+    d_values = mm(g_values[:CH, :].astype(bf16), perm, 1, 0)
+    planes = (
+        d_gates[:, :CH], d_values[:, :CH], d_gates[:, CH:], d_values[:, CH:],
+        gg_ref[:CH, :], gow_ref[...], sums, jnp.zeros((CH, CH), f32),
+    )
+    for n, plane in enumerate(planes):
+        pk_s[pl.ds(n, CH, stride=8), :] = plane
+    s_ref[...] = pk_s[...].astype(bf16).reshape(CH, 8, CH)
 
 
 def k5b(pair_ref, a_ref, sv_ref, sg_ref, dg_ref, ig_ref, w_ref, gw_ref, gp_ref, bk_s, v_s):
@@ -513,11 +514,10 @@
         k3,
         name="middle",
         compiler_params=SMALL,
-        grid=(STEPS,),
-        in_specs=[lanes(PEERS, OWN), lanes(CH), one, square],
-        out_specs=lanes(PEERS, OWN),
-        out_shape=out((PEERS, OWN, CELLS), bf16),
-        scratch_shapes=[vm(CH, STEP), vm(CH, CH)],
+        in_specs=[HERE] * 4,
+        out_specs=AWAY,
+        out_shape=away((PEERS, OWN, CELLS), bf16),
+        scratch_shapes=[vm(STEPS, CH, STEP), wb(PEERS, OWN, CELLS), pltpu.SemaphoreType.DMA((STEPS,))],
     )(product, d_out, out_gain, out_weight)
     d_product = swap(d_product, group)
     d_gate, g_out_weight, g_out, g_gate = pl.pallas_call(
@@ -539,12 +539,8 @@
         k5,
         name="weights",
         compiler_params=SMALL,
-        grid=(STEPS,),
-        in_specs=[
-            lanes(PEERS, 2 * OWN), lanes(2 * CH), lanes(2 * CH), lanes(CH + 16), one, one,
-            proj, square, square, whole(2, CH, CH), whole(CH + 16, CH),
-        ],
-        out_specs=whole(CH, 8, CH),
+        in_specs=[HERE] * 11,
+        out_specs=HERE,
         out_shape=out((CH, 8, CH), bf16),
         scratch_shapes=[vm(4 * CH, CH + 16), vm(CH * 8, CH)],
     )(d_factors, by_value, by_gate, normed, in_gain, in_bias, proj_weight, gate_weight,

time: 155 us -> 152 us (0.981)
  Pallas kernels: 41.9 us -> 39.3 us
    pallas_call x2, Pallas kernels: 6.44 us -> 3.9 us  [the longest x1 2.26 us: per_device(): pl.pallas_call(k3, name='middle', compiler_params=SMALL, in_specs=[HERE]...]
where the time goes in v4:
time: 152 us; the launch traced here: 151 us
  blocking collectives  65.4 us (43%)
  Pallas kernels  39.3 us (26%)
  waiting for transfers between devices  26.5 us (17%)
  starting transfers between devices  18.4 us (12%)
    all_to_all x1, blocking collectives, per_device(): d_factors = swap(d_factors, group)  27.9 us
    all_to_all x1, blocking collectives, per_device(): parts = swap(packed, everyone)  19.1 us
    all_to_all x1, blocking collectives, per_device(): product = swap(product, group)  18.4 us
    all_to_all x1, waiting for transfers between devices, per_device(): factors = swap(factors, group)  14.8 us
    all_to_all x1, starting transfers between devices, per_device(): factors = swap(factors, group)  8.57 us
    pallas_call x1, Pallas kernels, per_device(): pl.pallas_call(k1b, name='gate', compiler_params=SMALL, grid=(STEPS,), in...  7.43 us
    all_to_all x1, waiting for transfers between devices, per_device(): d_product = swap(d_product, group)  7.26 us
    pallas_call x1, Pallas kernels, per_device(): pl.pallas_call(k5b, name='inputs', compiler_params=SMALL, grid=(STEPS,),...  6.66 us
  transfers between devices with their start and end apart: 3, of which 3 were waited for; matrix products, arithmetic and copies ran while one was open for 0% of the time, Pallas kernels for 13%

profile of v4, /device:TPU:1, one launch (start us, length us, event | category | flops | bytes accessed | tf_op | source)
XLA Modules:
  0.0 151.1 jit_solution(769450906572636667)
XLA Ops:
  1.3 5.8 %factors.1 = bf16[32,8,3200]{2,1,0:T(8,128)(2,1)} custom-call(s32[1]{0:T(128)S(6)} %copy.18.crop_ref, f32[80,40,128]{2,1,0:T(8,128)} %bitcast.20, f32[1,128]{1,0:T(1,128)} %bitcast.11, f32[1,128]{1,0:T(1,128)} %bitcast.15, bf16[128,512]{1,0:T(8,128)(2,1)} %w_ref.7), custom_call_target="tpu_custom_call" | custom-call | tf_op jit(solution)/shard_map/factors/pallas_call | solution.py:486
  7.0 8.6 %all-to-all-start = ((bf16[32,8,3200]{2,1,0:T(8,128)(2,1)}), bf16[32,8,3200]{2,1,0:T(8,128)(2,1)S(1)}, u32[]{:S(2)}, u32[]{:S(2)}) async-start(bf16[32,8,3200]{2,1,0:T(8,128)(2,1)} %factors.1), calls=%async_computation | async-start | bytes 3276800 | tf_op jit(solution)/shard_map/all_to_all | solution.py:496
  15.6 7.4 %gate.1 = (bf16[144,3200]{1,0:T(8,128)(2,1)}, bf16[128,3200]{1,0:T(8,128)(2,1)}, f32[128,3200]{1,0:T(8,128)}, bf16[256,3200]{1,0:T(8,128)(2,1)}, bf16[256,3200]{1,0:T(8,128)(2,1)}) custom-call(s32[1]{0:T(128)S(6)} %copy.18.crop_ref, f32[80,40,128]{2,1,0:T(8,128)} %bitcast.21, f32[80,40,128]{2,1,0:T(8,128)} %bitcast.25, f32[1,128]{1,0:T(1,128)} %bitcast.12, ...), custom_call_target="tpu_custom_call" | custom-call | flops 1000000000 | bytes 8000000 | tf_op jit(solution)/shard_map/gate/pallas_call | solution.py:497
  23.0 14.8 %all-to-all-done.y_ref = bf16[32,8,3200]{2,1,0:T(8,128)(2,1)S(1)} async-done(((bf16[32,8,3200]{2,1,0:T(8,128)(2,1)}), bf16[32,8,3200]{2,1,0:T(8,128)(2,1)S(1)}, u32[]{:S(2)}, u32[]{:S(2)}) %all-to-all-start) | async-done | bytes 1638432 | tf_op jit(solution)/shard_map/all_to_all | solution.py:496
  37.8 0.0 copy-start
  37.8 0.0 copy-start.5
  37.8 0.0 copy-start.12
  37.8 3.5 %product.1 = (bf16[4,320,512]{2,1,0:T(8,128)(2,1)}, bf16[4,320,512]{2,1,0:T(8,128)(2,1)}, bf16[32,4,3200]{2,1,0:T(4,128)(2,1)S(1)}) custom-call(bf16[32,8,3200]{2,1,0:T(8,128)(2,1)S(1)} %all-to-all-done.y_ref, bf16[128,3200]{1,0:T(8,128)(2,1)} %get-tuple-element.27._.do_ref), custom_call_target="tpu_custom_call" | custom-call | tf_op jit(solution)/shard_map/product/pallas_call | solution.py:436
  41.3 18.4 %all_to_all.30.z_ref = bf16[32,4,3200]{2,1,0:T(4,128)(2,1)S(1)} all-to-all(bf16[32,4,3200]{2,1,0:T(4,128)(2,1)S(1)} %get-tuple-element.28), channel_id=1, replica_groups=mesh['samp'=4,'row'=4,'col'=8] {'row','col'}, dimensions={0} | all-to-all | bytes 1638400 | tf_op jit(solution)/shard_map/all_to_all | solution.py:512
  59.8 0.0 copy-done
  59.8 0.0 copy-done.5
  59.8 0.0 copy-done.12
  59.8 2.3 %middle.1 = bf16[32,4,3200]{2,1,0:T(4,128)(2,1)} custom-call(bf16[32,4,3200]{2,1,0:T(4,128)(2,1)S(1)} %all_to_all.30.z_ref, bf16[128,3200]{1,0:T(8,128)(2,1)S(1)} %copy-done, f32[1,128]{1,0:T(1,128)S(1)} %bitcast.19, bf16[128,128]{1,0:T(8,128)(2,1)S(1)} %copy-done.5), custom_call_target="tpu_custom_call" | custom-call | tf_op jit(solution)/shard_map/middle/pallas_call | solution.py:513
  62.1 5.5 %all-to-all-start.2 = ((bf16[32,4,3200]{2,1,0:T(4,128)(2,1)}), bf16[32,4,3200]{2,1,0:T(4,128)(2,1)S(1)}, u32[]{:S(2)}, u32[]{:S(2)}) async-start(bf16[32,4,3200]{2,1,0:T(4,128)(2,1)} %middle.1), calls=%async_computation.2 | async-start | bytes 1638400 | tf_op jit(solution)/shard_map/all_to_all | solution.py:522
  67.6 6.1 %outputs.1 = (bf16[128,3200]{1,0:T(8,128)(2,1)}, f32[128,128]{1,0:T(8,128)}, f32[2,128,128]{2,1,0:T(8,128)}, f32[144,128]{1,0:T(8,128)}) custom-call(bf16[32,4,3200]{2,1,0:T(4,128)(2,1)S(1)} %all_to_all.30.z_ref, bf16[144,3200]{1,0:T(8,128)(2,1)} %get-tuple-element.31.n_ref, bf16[128,3200]{1,0:T(8,128)(2,1)} %get-tuple-element.27._.do_ref, ...), custom_call_target="tpu_custom_call" | custom-call | flops 1000000000 | bytes 8000000 | tf_op jit(solution)/shard_map/outputs/pallas_call | solution.py:523
  73.7 7.3 %all-to-all-done.2.dp_ref = bf16[32,4,3200]{2,1,0:T(4,128)(2,1)S(1)} async-done(((bf16[32,4,3200]{2,1,0:T(4,128)(2,1)}), bf16[32,4,3200]{2,1,0:T(4,128)(2,1)S(1)}, u32[]{:S(2)}, u32[]{:S(2)}) %all-to-all-start.2) | async-done | bytes 819232 | tf_op jit(solution)/shard_map/all_to_all | solution.py:522
  80.9 0.0 copy-start.3
  80.9 0.0 copy-start.4
  80.9 0.0 copy-start.6
  80.9 0.0 copy-start.7
  81.0 0.0 copy-start.8
  81.0 0.0 copy-start.9
  81.0 4.2 %slopes.1 = bf16[32,8,3200]{2,1,0:T(8,128)(2,1)S(1)} custom-call(bf16[32,4,3200]{2,1,0:T(4,128)(2,1)S(1)} %all-to-all-done.2.dp_ref, bf16[4,320,512]{2,1,0:T(8,128)(2,1)} %get-tuple-element.29.l_ref, bf16[4,320,512]{2,1,0:T(8,128)(2,1)} %get-tuple-element.30.r_ref, bf16[128,3200]{1,0:T(8,128)(2,1)} %get-tuple-element.33._.dg_ref), custom_call_target="tpu_custom_call" | custom-call | tf_op jit(solution)/shard_map/slopes/pallas_call | solution.py:451
  85.2 0.0 copy-start.1
  85.2 0.0 copy-start.2
  85.2 0.0 copy-start.10
  85.2 0.0 copy-start.11
  85.3 27.9 %all_to_all.31.a_ref = bf16[32,8,3200]{2,1,0:T(8,128)(2,1)S(1)} all-to-all(bf16[32,8,3200]{2,1,0:T(8,128)(2,1)S(1)} %slopes.1), channel_id=1, replica_groups=mesh['samp'=4,'row'=4,'col'=8] {'row','col'}, dimensions={0} | all-to-all | bytes 3276800 | tf_op jit(solution)/shard_map/all_to_all | solution.py:537
  113.2 0.0 copy-done.3
  113.2 0.0 copy-done.4
  113.2 0.0 copy-done.6
  113.2 0.0 copy-done.7
  113.2 0.0 copy-done.8
  113.2 0.0 copy-done.9
  113.2 0.0 copy-done.1
  113.2 0.0 copy-done.2
  113.2 0.0 copy-done.10
  113.2 0.0 copy-done.11
  113.2 1.6 %weights.1 = bf16[128,8,128]{2,1,0:T(8,128)(2,1)S(1)} custom-call(bf16[32,8,3200]{2,1,0:T(8,128)(2,1)S(1)} %all_to_all.31.a_ref, bf16[256,3200]{1,0:T(8,128)(2,1)S(1)} %copy-done.1, bf16[256,3200]{1,0:T(8,128)(2,1)S(1)} %copy-done.2, bf16[144,3200]{1,0:T(8,128)(2,1)S(1)} %copy-done.3, f32[1,128]{1,0:T(1,128)S(1)} %bitcast.14, f32[1,128]{1,0:T(1,128)S(1)} %bitcast.17, ...), custom_call_target="tpu_custom_call" | custom-call | tf_op jit(solution)/shard_map/weights/pallas_call | solution.py:538
  114.9 19.1 %all_to_all.32.x_ref = bf16[128,8,128]{2,1,0:T(8,128)(2,1)S(1)} all-to-all(bf16[128,8,128]{2,1,0:T(8,128)(2,1)S(1)} %weights.1), channel_id=1, replica_groups=mesh['samp'=4,'row'=4,'col'=8] {'samp','row','col'}, dimensions={0} | all-to-all | bytes 524288 | tf_op jit(solution)/shard_map/all_to_all | solution.py:548
  134.0 0.9 total.1
  134.8 4.4 %all-to-all-start.5 = ((bf16[128,8,128]{2,1,0:T(8,128)(2,1)}), bf16[128,8,128]{2,1,0:T(8,128)(2,1)S(1)}, u32[]{:S(2)}, u32[]{:S(2)}) async-start(bf16[128,8,128]{2,1,0:T(8,128)(2,1)} %total.1), calls=%async_computation.5 | async-start | bytes 524288 | tf_op jit(solution)/shard_map/all_to_all | solution.py:563
  139.2 6.7 %inputs.1 = f32[80,40,128]{2,1,0:T(8,128)} custom-call(f32[80,40,128]{2,1,0:T(8,128)} %bitcast.22, bf16[32,8,3200]{2,1,0:T(8,128)(2,1)S(1)} %all_to_all.31.a_ref, bf16[256,3200]{1,0:T(8,128)(2,1)} %get-tuple-element.34.sv_ref, bf16[256,3200]{1,0:T(8,128)(2,1)} %get-tuple-element.35.sg_ref, bf16[128,3200]{1,0:T(8,128)(2,1)} %get-tuple-element.33._.dg_ref, ...), custom_call_target="tpu_custom_call" | custom-call | flops 1000000000 | bytes 8000000 | tf_op jit(solution)/shard_map/inputs/pallas_call | solution.py:549
  145.8 4.4 %all-to-all-done.5.x_ref = bf16[128,8,128]{2,1,0:T(8,128)(2,1)S(1)} async-done(((bf16[128,8,128]{2,1,0:T(8,128)(2,1)}), bf16[128,8,128]{2,1,0:T(8,128)(2,1)S(1)}, u32[]{:S(2)}, u32[]{:S(2)}) %all-to-all-start.5) | async-done | bytes 262176 | tf_op jit(solution)/shard_map/all_to_all | solution.py:563
  150.3 0.9 unpack.1
Async XLA Ops:
  7.0 30.8 %all-to-all-start = ((bf16[32,8,3200]{2,1,0:T(8,128)(2,1)}), bf16[32,8,3200]{2,1,0:T(8,128)(2,1)S(1)}, u32[]{:S(2)}, u32[]{:S(2)}) async-start(bf16[32,8,3200]{2,1,0:T(8,128)(2,1)} %factors.1), calls=%async_computation | async-start | bytes 3276800 | tf_op jit(solution)/shard_map/all_to_all | solution.py:496
  37.8 22.0 %copy-start = (bf16[128,3200]{1,0:T(8,128)(2,1)S(1)}, bf16[128,3200]{1,0:T(8,128)(2,1)}, u32[]{:S(2)}) copy-start(bf16[128,3200]{1,0:T(8,128)(2,1)} %get-tuple-element.27._.do_ref) | copy-start | bytes 2457604
  37.8 22.0 %copy-start.5 = (bf16[128,128]{1,0:T(8,128)(2,1)S(1)}, bf16[128,128]{1,0:T(8,128)(2,1)}, u32[]{:S(2)}) copy-start(bf16[128,128]{1,0:T(8,128)(2,1)} %ow_ref.3) | copy-start | bytes 98308
  37.8 22.0 %copy-start.12 = (f32[128]{0:T(128)S(1)}, f32[128]{0:T(128)}, u32[]{:S(2)}) copy-start(f32[128]{0:T(128)} %param.17) | copy-start | bytes 1540
  62.1 18.9 %all-to-all-start.2 = ((bf16[32,4,3200]{2,1,0:T(4,128)(2,1)}), bf16[32,4,3200]{2,1,0:T(4,128)(2,1)S(1)}, u32[]{:S(2)}, u32[]{:S(2)}) async-start(bf16[32,4,3200]{2,1,0:T(4,128)(2,1)} %middle.1), calls=%async_computation.2 | async-start | bytes 1638400 | tf_op jit(solution)/shard_map/all_to_all | solution.py:522
  80.9 32.2 %copy-start.3 = (bf16[144,3200]{1,0:T(8,128)(2,1)S(1)}, bf16[144,3200]{1,0:T(8,128)(2,1)}, u32[]{:S(2)}) copy-start(bf16[144,3200]{1,0:T(8,128)(2,1)} %get-tuple-element.31.n_ref) | copy-start | bytes 2764804
  80.9 32.2 %copy-start.4 = (bf16[128,512]{1,0:T(8,128)(2,1)S(1)}, bf16[128,512]{1,0:T(8,128)(2,1)}, u32[]{:S(2)}) copy-start(bf16[128,512]{1,0:T(8,128)(2,1)} %w_ref.7) | copy-start | bytes 393220
  80.9 32.2 %copy-start.6 = (bf16[128,128]{1,0:T(8,128)(2,1)S(1)}, bf16[128,128]{1,0:T(8,128)(2,1)}, u32[]{:S(2)}) copy-start(bf16[128,128]{1,0:T(8,128)(2,1)} %gw_ref.5) | copy-start | bytes 98308
  80.9 32.2 %copy-start.7 = (f32[2,128,128]{2,1,0:T(8,128)S(1)}, f32[2,128,128]{2,1,0:T(8,128)}, u32[]{:S(2)}) copy-start(f32[2,128,128]{2,1,0:T(8,128)} %get-tuple-element.37.gv_ref) | copy-start | bytes 393220
  81.0 32.2 %copy-start.8 = (f32[144,128]{1,0:T(8,128)S(1)}, f32[144,128]{1,0:T(8,128)}, u32[]{:S(2)}) copy-start(f32[144,128]{1,0:T(8,128)} %get-tuple-element.38.gg_ref) | copy-start | bytes 221188
  81.0 32.2 %copy-start.9 = (f32[128,128]{1,0:T(8,128)S(1)}, f32[128,128]{1,0:T(8,128)}, u32[]{:S(2)}) copy-start(f32[128,128]{1,0:T(8,128)} %get-tuple-element.36.gow_ref) | copy-start | bytes 196612
  85.2 28.0 %copy-start.1 = (bf16[256,3200]{1,0:T(8,128)(2,1)S(1)}, bf16[256,3200]{1,0:T(8,128)(2,1)}, u32[]{:S(2)}) copy-start(bf16[256,3200]{1,0:T(8,128)(2,1)} %get-tuple-element.34.sv_ref) | copy-start | bytes 4915204
  85.2 28.0 %copy-start.2 = (bf16[256,3200]{1,0:T(8,128)(2,1)S(1)}, bf16[256,3200]{1,0:T(8,128)(2,1)}, u32[]{:S(2)}) copy-start(bf16[256,3200]{1,0:T(8,128)(2,1)} %get-tuple-element.35.sg_ref) | copy-start | bytes 4915204
  85.2 28.0 %copy-start.10 = (f32[128]{0:T(128)S(1)}, f32[128]{0:T(128)}, u32[]{:S(2)}) copy-start(f32[128]{0:T(128)} %param.13) | copy-start | bytes 1540
  85.2 28.0 %copy-start.11 = (f32[128]{0:T(128)S(1)}, f32[128]{0:T(128)}, u32[]{:S(2)}) copy-start(f32[128]{0:T(128)} %param.14) | copy-start | bytes 1540
  134.8 15.4 %all-to-all-start.5 = ((bf16[128,8,128]{2,1,0:T(8,128)(2,1)}), bf16[128,8,128]{2,1,0:T(8,128)(2,1)S(1)}, u32[]{:S(2)}, u32[]{:S(2)}) async-start(bf16[128,8,128]{2,1,0:T(8,128)(2,1)} %total.1), calls=%async_computation.5 | async-start | bytes 524288 | tf_op jit(solution)/shard_map/all_to_all | solution.py:563

commit v5 on v4

--- a/solution.py
+++ b/solution.py
@@ -376,7 +376,7 @@
         flat[pl.ds(k, TALL, stride=8), :] = back[k * TALL : (k + 1) * TALL, :]
 
 
-def k6(x_ref, o_ref):
+def k6(x_ref, _, o_ref):
     total = jnp.sum(x_ref[...].astype(f32), axis=0).astype(bf16)
     o_ref[...] = jnp.broadcast_to(total[None], o_ref.shape)
 
@@ -559,7 +559,14 @@
         scratch_shapes=[wb(CH, 5 * CH), vm(CH, CH)],
         cost_estimate=cost,
     )(*keep_away(pair), d_factors, *keep_away(by_value, by_gate, d_gate, in_gain, proj_weight, gate_weight))
-    total = pl.pallas_call(k6, name="total", compiler_params=SMALL, out_shape=out((CH, 8, CH), bf16))(parts)
+    total = pl.pallas_call(
+        k6,
+        name="total",
+        compiler_params=SMALL,
+        in_specs=[HERE, AWAY],
+        out_specs=HERE,
+        out_shape=out((CH, 8, CH), bf16),
+    )(parts, *keep_away(grad_pair))
     total = swap(total, everyone)
     g_proj_weight, g_gate_weight, g_out_weight, *sums = pl.pallas_call(
         functools.partial(k7, factor=1.0 / FULL),

time: 152 us -> 153 us (level)
  starting transfers between devices: 18.4 us -> 22.2 us
  blocking collectives: 65.4 us -> 62.6 us
    all_to_all x1, starting transfers between devices: 4.35 us -> 8.18 us  [per_device(): parts = swap(packed, everyone)]
    all_to_all x1, blocking collectives: 19.1 us -> 16.2 us  [per_device(): total = swap(total, everyone)]
where the time goes in v5:
time: 153 us; the launch traced here: 152 us
  blocking collectives  62.6 us (41%)
  Pallas kernels  39.3 us (26%)
  waiting for transfers between devices  26.5 us (17%)
  starting transfers between devices  22.2 us (15%)
    all_to_all x1, blocking collectives, per_device(): d_factors = swap(d_factors, group)  27.9 us
    all_to_all x1, blocking collectives, per_device(): product = swap(product, group)  18.4 us
    all_to_all x1, blocking collectives, per_device(): total = swap(total, everyone)  16.2 us
    all_to_all x1, waiting for transfers between devices, per_device(): factors = swap(factors, group)  14.8 us
    all_to_all x1, starting transfers between devices, per_device(): factors = swap(factors, group)  8.57 us
    all_to_all x1, starting transfers between devices, per_device(): parts = swap(packed, everyone)  8.18 us
    pallas_call x1, Pallas kernels, per_device(): pl.pallas_call(k1b, name='gate', compiler_params=SMALL, grid=(STEPS,), in...  7.43 us
    all_to_all x1, waiting for transfers between devices, per_device(): d_product = swap(d_product, group)  7.26 us
  transfers between devices with their start and end apart: 3, of which 3 were waited for; matrix products, arithmetic and copies ran while one was open for 0% of the time, Pallas kernels for 13%

profile of v5, /device:TPU:1, one launch (start us, length us, event | category | flops | bytes accessed | tf_op | source)
XLA Modules:
  0.0 152.1 jit_solution(9155224842447440986)
XLA Ops:
  1.3 5.8 %factors.1 = bf16[32,8,3200]{2,1,0:T(8,128)(2,1)} custom-call(s32[1]{0:T(128)S(6)} %copy.18.crop_ref, f32[80,40,128]{2,1,0:T(8,128)} %bitcast.21, f32[1,128]{1,0:T(1,128)} %bitcast.11, f32[1,128]{1,0:T(1,128)} %bitcast.15, bf16[128,512]{1,0:T(8,128)(2,1)} %w_ref.7), custom_call_target="tpu_custom_call" | custom-call | tf_op jit(solution)/shard_map/factors/pallas_call | solution.py:486
  7.0 8.6 %all-to-all-start = ((bf16[32,8,3200]{2,1,0:T(8,128)(2,1)}), bf16[32,8,3200]{2,1,0:T(8,128)(2,1)S(1)}, u32[]{:S(2)}, u32[]{:S(2)}) async-start(bf16[32,8,3200]{2,1,0:T(8,128)(2,1)} %factors.1), calls=%async_computation | async-start | bytes 3276800 | tf_op jit(solution)/shard_map/all_to_all | solution.py:496
  15.6 7.4 %gate.1 = (bf16[144,3200]{1,0:T(8,128)(2,1)}, bf16[128,3200]{1,0:T(8,128)(2,1)}, f32[128,3200]{1,0:T(8,128)}, bf16[256,3200]{1,0:T(8,128)(2,1)}, bf16[256,3200]{1,0:T(8,128)(2,1)}) custom-call(s32[1]{0:T(128)S(6)} %copy.18.crop_ref, f32[80,40,128]{2,1,0:T(8,128)} %bitcast.22, f32[80,40,128]{2,1,0:T(8,128)} %bitcast.25, f32[1,128]{1,0:T(1,128)} %bitcast.12, ...), custom_call_target="tpu_custom_call" | custom-call | flops 1000000000 | bytes 8000000 | tf_op jit(solution)/shard_map/gate/pallas_call | solution.py:497
  23.0 14.8 %all-to-all-done.y_ref = bf16[32,8,3200]{2,1,0:T(8,128)(2,1)S(1)} async-done(((bf16[32,8,3200]{2,1,0:T(8,128)(2,1)}), bf16[32,8,3200]{2,1,0:T(8,128)(2,1)S(1)}, u32[]{:S(2)}, u32[]{:S(2)}) %all-to-all-start) | async-done | bytes 1638432 | tf_op jit(solution)/shard_map/all_to_all | solution.py:496
  37.8 0.0 copy-start
  37.8 0.0 copy-start.5
  37.8 0.0 copy-start.12
  37.8 3.5 %product.1 = (bf16[4,320,512]{2,1,0:T(8,128)(2,1)}, bf16[4,320,512]{2,1,0:T(8,128)(2,1)}, bf16[32,4,3200]{2,1,0:T(4,128)(2,1)S(1)}) custom-call(bf16[32,8,3200]{2,1,0:T(8,128)(2,1)S(1)} %all-to-all-done.y_ref, bf16[128,3200]{1,0:T(8,128)(2,1)} %get-tuple-element.27._.do_ref), custom_call_target="tpu_custom_call" | custom-call | tf_op jit(solution)/shard_map/product/pallas_call | solution.py:436
  41.3 18.4 %all_to_all.30.z_ref = bf16[32,4,3200]{2,1,0:T(4,128)(2,1)S(1)} all-to-all(bf16[32,4,3200]{2,1,0:T(4,128)(2,1)S(1)} %get-tuple-element.28), channel_id=1, replica_groups=mesh['samp'=4,'row'=4,'col'=8] {'row','col'}, dimensions={0} | all-to-all | bytes 1638400 | tf_op jit(solution)/shard_map/all_to_all | solution.py:512
  59.8 0.0 copy-done
  59.8 0.0 copy-done.5
  59.8 0.0 copy-done.12
  59.8 2.3 %middle.1 = bf16[32,4,3200]{2,1,0:T(4,128)(2,1)} custom-call(bf16[32,4,3200]{2,1,0:T(4,128)(2,1)S(1)} %all_to_all.30.z_ref, bf16[128,3200]{1,0:T(8,128)(2,1)S(1)} %copy-done, f32[1,128]{1,0:T(1,128)S(1)} %bitcast.19, bf16[128,128]{1,0:T(8,128)(2,1)S(1)} %copy-done.5), custom_call_target="tpu_custom_call" | custom-call | tf_op jit(solution)/shard_map/middle/pallas_call | solution.py:513
  62.1 5.5 %all-to-all-start.2 = ((bf16[32,4,3200]{2,1,0:T(4,128)(2,1)}), bf16[32,4,3200]{2,1,0:T(4,128)(2,1)S(1)}, u32[]{:S(2)}, u32[]{:S(2)}) async-start(bf16[32,4,3200]{2,1,0:T(4,128)(2,1)} %middle.1), calls=%async_computation.2 | async-start | bytes 1638400 | tf_op jit(solution)/shard_map/all_to_all | solution.py:522
  67.6 6.1 %outputs.1 = (bf16[128,3200]{1,0:T(8,128)(2,1)}, f32[128,128]{1,0:T(8,128)}, f32[2,128,128]{2,1,0:T(8,128)}, f32[144,128]{1,0:T(8,128)}) custom-call(bf16[32,4,3200]{2,1,0:T(4,128)(2,1)S(1)} %all_to_all.30.z_ref, bf16[144,3200]{1,0:T(8,128)(2,1)} %get-tuple-element.31.n_ref, bf16[128,3200]{1,0:T(8,128)(2,1)} %get-tuple-element.27._.do_ref, ...), custom_call_target="tpu_custom_call" | custom-call | flops 1000000000 | bytes 8000000 | tf_op jit(solution)/shard_map/outputs/pallas_call | solution.py:523
  73.7 7.3 %all-to-all-done.2.dp_ref = bf16[32,4,3200]{2,1,0:T(4,128)(2,1)S(1)} async-done(((bf16[32,4,3200]{2,1,0:T(4,128)(2,1)}), bf16[32,4,3200]{2,1,0:T(4,128)(2,1)S(1)}, u32[]{:S(2)}, u32[]{:S(2)}) %all-to-all-start.2) | async-done | bytes 819232 | tf_op jit(solution)/shard_map/all_to_all | solution.py:522
  80.9 0.0 copy-start.3
  80.9 0.0 copy-start.4
  80.9 0.0 copy-start.6
  80.9 0.0 copy-start.7
  81.0 0.0 copy-start.8
  81.0 0.0 copy-start.9
  81.0 4.2 %slopes.1 = bf16[32,8,3200]{2,1,0:T(8,128)(2,1)S(1)} custom-call(bf16[32,4,3200]{2,1,0:T(4,128)(2,1)S(1)} %all-to-all-done.2.dp_ref, bf16[4,320,512]{2,1,0:T(8,128)(2,1)} %get-tuple-element.29.l_ref, bf16[4,320,512]{2,1,0:T(8,128)(2,1)} %get-tuple-element.30.r_ref, bf16[128,3200]{1,0:T(8,128)(2,1)} %get-tuple-element.33._.dg_ref), custom_call_target="tpu_custom_call" | custom-call | tf_op jit(solution)/shard_map/slopes/pallas_call | solution.py:451
  85.2 0.0 copy-start.1
  85.2 0.0 copy-start.2
  85.2 0.0 copy-start.10
  85.2 0.0 copy-start.11
  85.3 27.9 %all_to_all.31.a_ref = bf16[32,8,3200]{2,1,0:T(8,128)(2,1)S(1)} all-to-all(bf16[32,8,3200]{2,1,0:T(8,128)(2,1)S(1)} %slopes.1), channel_id=1, replica_groups=mesh['samp'=4,'row'=4,'col'=8] {'row','col'}, dimensions={0} | all-to-all | bytes 3276800 | tf_op jit(solution)/shard_map/all_to_all | solution.py:537
  113.2 0.0 copy-done.3
  113.2 0.0 copy-done.4
  113.2 0.0 copy-done.6
  113.2 0.0 copy-done.7
  113.2 0.0 copy-done.8
  113.2 0.0 copy-done.9
  113.2 0.0 copy-done.1
  113.2 0.0 copy-done.2
  113.2 0.0 copy-done.10
  113.2 0.0 copy-done.11
  113.2 2.3 %weights.1 = bf16[128,8,128]{2,1,0:T(8,128)(2,1)} custom-call(bf16[32,8,3200]{2,1,0:T(8,128)(2,1)S(1)} %all_to_all.31.a_ref, bf16[256,3200]{1,0:T(8,128)(2,1)S(1)} %copy-done.1, bf16[256,3200]{1,0:T(8,128)(2,1)S(1)} %copy-done.2, bf16[144,3200]{1,0:T(8,128)(2,1)S(1)} %copy-done.3, f32[1,128]{1,0:T(1,128)S(1)} %bitcast.14, f32[1,128]{1,0:T(1,128)S(1)} %bitcast.17, ...), custom_call_target="tpu_custom_call" | custom-call | tf_op jit(solution)/shard_map/weights/pallas_call | solution.py:538
  115.6 8.2 %all-to-all-start.4 = ((bf16[128,8,128]{2,1,0:T(8,128)(2,1)}), bf16[128,8,128]{2,1,0:T(8,128)(2,1)S(1)}, u32[]{:S(2)}, u32[]{:S(2)}) async-start(bf16[128,8,128]{2,1,0:T(8,128)(2,1)} %weights.1), calls=%async_computation.4 | async-start | bytes 524288 | tf_op jit(solution)/shard_map/all_to_all | solution.py:548
  123.8 6.7 %inputs.1._ = f32[80,40,128]{2,1,0:T(8,128)} custom-call(f32[80,40,128]{2,1,0:T(8,128)} %bitcast.23, bf16[32,8,3200]{2,1,0:T(8,128)(2,1)S(1)} %all_to_all.31.a_ref, bf16[256,3200]{1,0:T(8,128)(2,1)} %get-tuple-element.34.sv_ref, bf16[256,3200]{1,0:T(8,128)(2,1)} %get-tuple-element.35.sg_ref, bf16[128,3200]{1,0:T(8,128)(2,1)} %get-tuple-element.33._.dg_ref, ...), custom_call_target="tpu_custom_call" | custom-call | flops 1000000000 | bytes 8000000 | tf_op jit(solution)/shard_map/inputs/pallas_call | solution.py:549
  130.4 4.4 %all-to-all-done.4.x_ref = bf16[128,8,128]{2,1,0:T(8,128)(2,1)S(1)} async-done(((bf16[128,8,128]{2,1,0:T(8,128)(2,1)}), bf16[128,8,128]{2,1,0:T(8,128)(2,1)S(1)}, u32[]{:S(2)}, u32[]{:S(2)}) %all-to-all-start.4) | async-done | bytes 262176 | tf_op jit(solution)/shard_map/all_to_all | solution.py:548
  134.9 0.2 total.1
  135.0 16.2 %all_to_all.32.x_ref = bf16[128,8,128]{2,1,0:T(8,128)(2,1)S(1)} all-to-all(bf16[128,8,128]{2,1,0:T(8,128)(2,1)S(1)} %total.1), channel_id=1, replica_groups=mesh['samp'=4,'row'=4,'col'=8] {'samp','row','col'}, dimensions={0} | all-to-all | bytes 524288 | tf_op jit(solution)/shard_map/all_to_all | solution.py:570
  151.3 0.9 unpack.1
Async XLA Ops:
  7.0 30.8 %all-to-all-start = ((bf16[32,8,3200]{2,1,0:T(8,128)(2,1)}), bf16[32,8,3200]{2,1,0:T(8,128)(2,1)S(1)}, u32[]{:S(2)}, u32[]{:S(2)}) async-start(bf16[32,8,3200]{2,1,0:T(8,128)(2,1)} %factors.1), calls=%async_computation | async-start | bytes 3276800 | tf_op jit(solution)/shard_map/all_to_all | solution.py:496
  37.8 22.0 %copy-start = (bf16[128,3200]{1,0:T(8,128)(2,1)S(1)}, bf16[128,3200]{1,0:T(8,128)(2,1)}, u32[]{:S(2)}) copy-start(bf16[128,3200]{1,0:T(8,128)(2,1)} %get-tuple-element.27._.do_ref) | copy-start | bytes 2457604
  37.8 22.0 %copy-start.5 = (bf16[128,128]{1,0:T(8,128)(2,1)S(1)}, bf16[128,128]{1,0:T(8,128)(2,1)}, u32[]{:S(2)}) copy-start(bf16[128,128]{1,0:T(8,128)(2,1)} %ow_ref.3) | copy-start | bytes 98308
  37.8 22.0 %copy-start.12 = (f32[128]{0:T(128)S(1)}, f32[128]{0:T(128)}, u32[]{:S(2)}) copy-start(f32[128]{0:T(128)} %param.17) | copy-start | bytes 1540
  62.1 18.9 %all-to-all-start.2 = ((bf16[32,4,3200]{2,1,0:T(4,128)(2,1)}), bf16[32,4,3200]{2,1,0:T(4,128)(2,1)S(1)}, u32[]{:S(2)}, u32[]{:S(2)}) async-start(bf16[32,4,3200]{2,1,0:T(4,128)(2,1)} %middle.1), calls=%async_computation.2 | async-start | bytes 1638400 | tf_op jit(solution)/shard_map/all_to_all | solution.py:522
  80.9 32.2 %copy-start.3 = (bf16[144,3200]{1,0:T(8,128)(2,1)S(1)}, bf16[144,3200]{1,0:T(8,128)(2,1)}, u32[]{:S(2)}) copy-start(bf16[144,3200]{1,0:T(8,128)(2,1)} %get-tuple-element.31.n_ref) | copy-start | bytes 2764804
  80.9 32.2 %copy-start.4 = (bf16[128,512]{1,0:T(8,128)(2,1)S(1)}, bf16[128,512]{1,0:T(8,128)(2,1)}, u32[]{:S(2)}) copy-start(bf16[128,512]{1,0:T(8,128)(2,1)} %w_ref.7) | copy-start | bytes 393220
  80.9 32.2 %copy-start.6 = (bf16[128,128]{1,0:T(8,128)(2,1)S(1)}, bf16[128,128]{1,0:T(8,128)(2,1)}, u32[]{:S(2)}) copy-start(bf16[128,128]{1,0:T(8,128)(2,1)} %gw_ref.5) | copy-start | bytes 98308
  80.9 32.2 %copy-start.7 = (f32[2,128,128]{2,1,0:T(8,128)S(1)}, f32[2,128,128]{2,1,0:T(8,128)}, u32[]{:S(2)}) copy-start(f32[2,128,128]{2,1,0:T(8,128)} %get-tuple-element.37.gv_ref) | copy-start | bytes 393220
  81.0 32.2 %copy-start.8 = (f32[144,128]{1,0:T(8,128)S(1)}, f32[144,128]{1,0:T(8,128)}, u32[]{:S(2)}) copy-start(f32[144,128]{1,0:T(8,128)} %get-tuple-element.38.gg_ref) | copy-start | bytes 221188
  81.0 32.2 %copy-start.9 = (f32[128,128]{1,0:T(8,128)S(1)}, f32[128,128]{1,0:T(8,128)}, u32[]{:S(2)}) copy-start(f32[128,128]{1,0:T(8,128)} %get-tuple-element.36.gow_ref) | copy-start | bytes 196612
  85.2 28.0 %copy-start.1 = (bf16[256,3200]{1,0:T(8,128)(2,1)S(1)}, bf16[256,3200]{1,0:T(8,128)(2,1)}, u32[]{:S(2)}) copy-start(bf16[256,3200]{1,0:T(8,128)(2,1)} %get-tuple-element.34.sv_ref) | copy-start | bytes 4915204
  85.2 28.0 %copy-start.2 = (bf16[256,3200]{1,0:T(8,128)(2,1)S(1)}, bf16[256,3200]{1,0:T(8,128)(2,1)}, u32[]{:S(2)}) copy-start(bf16[256,3200]{1,0:T(8,128)(2,1)} %get-tuple-element.35.sg_ref) | copy-start | bytes 4915204
  85.2 28.0 %copy-start.10 = (f32[128]{0:T(128)S(1)}, f32[128]{0:T(128)}, u32[]{:S(2)}) copy-start(f32[128]{0:T(128)} %param.13) | copy-start | bytes 1540
  85.2 28.0 %copy-start.11 = (f32[128]{0:T(128)S(1)}, f32[128]{0:T(128)}, u32[]{:S(2)}) copy-start(f32[128]{0:T(128)} %param.14) | copy-start | bytes 1540
  115.6 19.3 %all-to-all-start.4 = ((bf16[128,8,128]{2,1,0:T(8,128)(2,1)}), bf16[128,8,128]{2,1,0:T(8,128)(2,1)S(1)}, u32[]{:S(2)}, u32[]{:S(2)}) async-start(bf16[128,8,128]{2,1,0:T(8,128)(2,1)} %weights.1), calls=%async_computation.4 | async-start | bytes 524288 | tf_op jit(solution)/shard_map/all_to_all | solution.py:548

commit v6 on v4

--- a/solution.py
+++ b/solution.py
@@ -186,7 +186,7 @@
                 x_s[r, pl.ds(c * WIDE + g * 8 + k, 2 * OWN, stride=PITCH), :] = v
         return carry
 
-    lax.fori_loop(0, PEERS, spread, 0, unroll=8)
+    lax.fori_loop(0, PEERS, spread, 0, unroll=16)
     lane = lax.broadcasted_iota(jnp.int32, (FULL, 128), 1)
 
     def matrix(t):
@@ -214,7 +214,7 @@
             z_ref[s, :, g * STEP : (g + 1) * STEP] = fold(pieces).astype(bf16)
         return carry
 
-    lax.fori_loop(0, PEERS, gather, 0, unroll=8)
+    lax.fori_loop(0, PEERS, gather, 0, unroll=16)
     for copy in copies:
         copy.wait()
 

time: 152 us -> 152 us (level)
  no operation moved by 1% of the time
where the time goes in v6:
time: 152 us; the launch traced here: 151 us
  blocking collectives  65.4 us (43%)
  Pallas kernels  39.2 us (26%)
  waiting for transfers between devices  26.5 us (17%)
  starting transfers between devices  18.4 us (12%)
    all_to_all x1, blocking collectives, per_device(): d_factors = swap(d_factors, group)  27.9 us
    all_to_all x1, blocking collectives, per_device(): parts = swap(packed, everyone)  19 us
    all_to_all x1, blocking collectives, per_device(): product = swap(product, group)  18.4 us
    all_to_all x1, waiting for transfers between devices, per_device(): factors = swap(factors, group)  14.8 us
    all_to_all x1, starting transfers between devices, per_device(): factors = swap(factors, group)  8.57 us
    pallas_call x1, Pallas kernels, per_device(): pl.pallas_call(k1b, name='gate', compiler_params=SMALL, grid=(STEPS,), in...  7.43 us
    all_to_all x1, waiting for transfers between devices, per_device(): d_product = swap(d_product, group)  7.26 us
    pallas_call x1, Pallas kernels, per_device(): pl.pallas_call(k5b, name='inputs', compiler_params=SMALL, grid=(STEPS,),...  6.66 us
  transfers between devices with their start and end apart: 3, of which 3 were waited for; matrix products, arithmetic and copies ran while one was open for 0% of the time, Pallas kernels for 13%

profile of v6, /device:TPU:1, one launch (start us, length us, event | category | flops | bytes accessed | tf_op | source)
XLA Modules:
  0.0 151.0 jit_solution(13125196093499972168)
XLA Ops:
  1.3 5.8 %factors.1 = bf16[32,8,3200]{2,1,0:T(8,128)(2,1)} custom-call(s32[1]{0:T(128)S(6)} %copy.18.crop_ref, f32[80,40,128]{2,1,0:T(8,128)} %bitcast.20, f32[1,128]{1,0:T(1,128)} %bitcast.11, f32[1,128]{1,0:T(1,128)} %bitcast.15, bf16[128,512]{1,0:T(8,128)(2,1)} %w_ref.7), custom_call_target="tpu_custom_call" | custom-call | tf_op jit(solution)/shard_map/factors/pallas_call | solution.py:486
  7.0 8.6 %all-to-all-start = ((bf16[32,8,3200]{2,1,0:T(8,128)(2,1)}), bf16[32,8,3200]{2,1,0:T(8,128)(2,1)S(1)}, u32[]{:S(2)}, u32[]{:S(2)}) async-start(bf16[32,8,3200]{2,1,0:T(8,128)(2,1)} %factors.1), calls=%async_computation | async-start | bytes 3276800 | tf_op jit(solution)/shard_map/all_to_all | solution.py:496
  15.6 7.4 %gate.1 = (bf16[144,3200]{1,0:T(8,128)(2,1)}, bf16[128,3200]{1,0:T(8,128)(2,1)}, f32[128,3200]{1,0:T(8,128)}, bf16[256,3200]{1,0:T(8,128)(2,1)}, bf16[256,3200]{1,0:T(8,128)(2,1)}) custom-call(s32[1]{0:T(128)S(6)} %copy.18.crop_ref, f32[80,40,128]{2,1,0:T(8,128)} %bitcast.21, f32[80,40,128]{2,1,0:T(8,128)} %bitcast.25, f32[1,128]{1,0:T(1,128)} %bitcast.12, ...), custom_call_target="tpu_custom_call" | custom-call | flops 1000000000 | bytes 8000000 | tf_op jit(solution)/shard_map/gate/pallas_call | solution.py:497
  23.0 14.8 %all-to-all-done.y_ref = bf16[32,8,3200]{2,1,0:T(8,128)(2,1)S(1)} async-done(((bf16[32,8,3200]{2,1,0:T(8,128)(2,1)}), bf16[32,8,3200]{2,1,0:T(8,128)(2,1)S(1)}, u32[]{:S(2)}, u32[]{:S(2)}) %all-to-all-start) | async-done | bytes 1638432 | tf_op jit(solution)/shard_map/all_to_all | solution.py:496
  37.8 0.0 copy-start
  37.8 0.0 copy-start.5
  37.8 0.0 copy-start.12
  37.8 3.4 %product.1 = (bf16[4,320,512]{2,1,0:T(8,128)(2,1)}, bf16[4,320,512]{2,1,0:T(8,128)(2,1)}, bf16[32,4,3200]{2,1,0:T(4,128)(2,1)S(1)}) custom-call(bf16[32,8,3200]{2,1,0:T(8,128)(2,1)S(1)} %all-to-all-done.y_ref, bf16[128,3200]{1,0:T(8,128)(2,1)} %get-tuple-element.27._.do_ref), custom_call_target="tpu_custom_call" | custom-call | tf_op jit(solution)/shard_map/product/pallas_call | solution.py:436
  41.2 18.4 %all_to_all.30.z_ref = bf16[32,4,3200]{2,1,0:T(4,128)(2,1)S(1)} all-to-all(bf16[32,4,3200]{2,1,0:T(4,128)(2,1)S(1)} %get-tuple-element.28), channel_id=1, replica_groups=mesh['samp'=4,'row'=4,'col'=8] {'row','col'}, dimensions={0} | all-to-all | bytes 1638400 | tf_op jit(solution)/shard_map/all_to_all | solution.py:512
  59.7 0.0 copy-done
  59.7 0.0 copy-done.5
  59.7 0.0 copy-done.12
  59.7 2.3 %middle.1 = bf16[32,4,3200]{2,1,0:T(4,128)(2,1)} custom-call(bf16[32,4,3200]{2,1,0:T(4,128)(2,1)S(1)} %all_to_all.30.z_ref, bf16[128,3200]{1,0:T(8,128)(2,1)S(1)} %copy-done, f32[1,128]{1,0:T(1,128)S(1)} %bitcast.19, bf16[128,128]{1,0:T(8,128)(2,1)S(1)} %copy-done.5), custom_call_target="tpu_custom_call" | custom-call | tf_op jit(solution)/shard_map/middle/pallas_call | solution.py:513
  61.9 5.5 %all-to-all-start.2 = ((bf16[32,4,3200]{2,1,0:T(4,128)(2,1)}), bf16[32,4,3200]{2,1,0:T(4,128)(2,1)S(1)}, u32[]{:S(2)}, u32[]{:S(2)}) async-start(bf16[32,4,3200]{2,1,0:T(4,128)(2,1)} %middle.1), calls=%async_computation.2 | async-start | bytes 1638400 | tf_op jit(solution)/shard_map/all_to_all | solution.py:522
  67.4 6.1 %outputs.1 = (bf16[128,3200]{1,0:T(8,128)(2,1)}, f32[128,128]{1,0:T(8,128)}, f32[2,128,128]{2,1,0:T(8,128)}, f32[144,128]{1,0:T(8,128)}) custom-call(bf16[32,4,3200]{2,1,0:T(4,128)(2,1)S(1)} %all_to_all.30.z_ref, bf16[144,3200]{1,0:T(8,128)(2,1)} %get-tuple-element.31.n_ref, bf16[128,3200]{1,0:T(8,128)(2,1)} %get-tuple-element.27._.do_ref, ...), custom_call_target="tpu_custom_call" | custom-call | flops 1000000000 | bytes 8000000 | tf_op jit(solution)/shard_map/outputs/pallas_call | solution.py:523
  73.6 7.3 %all-to-all-done.2.dp_ref = bf16[32,4,3200]{2,1,0:T(4,128)(2,1)S(1)} async-done(((bf16[32,4,3200]{2,1,0:T(4,128)(2,1)}), bf16[32,4,3200]{2,1,0:T(4,128)(2,1)S(1)}, u32[]{:S(2)}, u32[]{:S(2)}) %all-to-all-start.2) | async-done | bytes 819232 | tf_op jit(solution)/shard_map/all_to_all | solution.py:522
  80.8 0.0 copy-start.3
  80.8 0.0 copy-start.4
  80.8 0.0 copy-start.6
  80.8 0.0 copy-start.7
  80.8 0.0 copy-start.8
  80.8 0.0 copy-start.9
  80.9 4.2 %slopes.1 = bf16[32,8,3200]{2,1,0:T(8,128)(2,1)S(1)} custom-call(bf16[32,4,3200]{2,1,0:T(4,128)(2,1)S(1)} %all-to-all-done.2.dp_ref, bf16[4,320,512]{2,1,0:T(8,128)(2,1)} %get-tuple-element.29.l_ref, bf16[4,320,512]{2,1,0:T(8,128)(2,1)} %get-tuple-element.30.r_ref, bf16[128,3200]{1,0:T(8,128)(2,1)} %get-tuple-element.33._.dg_ref), custom_call_target="tpu_custom_call" | custom-call | tf_op jit(solution)/shard_map/slopes/pallas_call | solution.py:451
  85.1 0.0 copy-start.1
  85.1 0.0 copy-start.2
  85.1 0.0 copy-start.10
  85.1 0.0 copy-start.11
  85.1 27.9 %all_to_all.31.a_ref = bf16[32,8,3200]{2,1,0:T(8,128)(2,1)S(1)} all-to-all(bf16[32,8,3200]{2,1,0:T(8,128)(2,1)S(1)} %slopes.1), channel_id=1, replica_groups=mesh['samp'=4,'row'=4,'col'=8] {'row','col'}, dimensions={0} | all-to-all | bytes 3276800 | tf_op jit(solution)/shard_map/all_to_all | solution.py:537
  113.0 0.0 copy-done.3
  113.0 0.0 copy-done.4
  113.0 0.0 copy-done.6
  113.0 0.0 copy-done.7
  113.1 0.0 copy-done.8
  113.1 0.0 copy-done.9
  113.1 0.0 copy-done.1
  113.1 0.0 copy-done.2
  113.1 0.0 copy-done.10
  113.1 0.0 copy-done.11
  113.1 1.7 %weights.1 = bf16[128,8,128]{2,1,0:T(8,128)(2,1)S(1)} custom-call(bf16[32,8,3200]{2,1,0:T(8,128)(2,1)S(1)} %all_to_all.31.a_ref, bf16[256,3200]{1,0:T(8,128)(2,1)S(1)} %copy-done.1, bf16[256,3200]{1,0:T(8,128)(2,1)S(1)} %copy-done.2, bf16[144,3200]{1,0:T(8,128)(2,1)S(1)} %copy-done.3, f32[1,128]{1,0:T(1,128)S(1)} %bitcast.14, f32[1,128]{1,0:T(1,128)S(1)} %bitcast.17, ...), custom_call_target="tpu_custom_call" | custom-call | tf_op jit(solution)/shard_map/weights/pallas_call | solution.py:538
  114.8 19.0 %all_to_all.32.x_ref = bf16[128,8,128]{2,1,0:T(8,128)(2,1)S(1)} all-to-all(bf16[128,8,128]{2,1,0:T(8,128)(2,1)S(1)} %weights.1), channel_id=1, replica_groups=mesh['samp'=4,'row'=4,'col'=8] {'samp','row','col'}, dimensions={0} | all-to-all | bytes 524288 | tf_op jit(solution)/shard_map/all_to_all | solution.py:548
  133.8 0.9 total.1
  134.7 4.4 %all-to-all-start.5 = ((bf16[128,8,128]{2,1,0:T(8,128)(2,1)}), bf16[128,8,128]{2,1,0:T(8,128)(2,1)S(1)}, u32[]{:S(2)}, u32[]{:S(2)}) async-start(bf16[128,8,128]{2,1,0:T(8,128)(2,1)} %total.1), calls=%async_computation.5 | async-start | bytes 524288 | tf_op jit(solution)/shard_map/all_to_all | solution.py:563
  139.0 6.7 %inputs.1 = f32[80,40,128]{2,1,0:T(8,128)} custom-call(f32[80,40,128]{2,1,0:T(8,128)} %bitcast.22, bf16[32,8,3200]{2,1,0:T(8,128)(2,1)S(1)} %all_to_all.31.a_ref, bf16[256,3200]{1,0:T(8,128)(2,1)} %get-tuple-element.34.sv_ref, bf16[256,3200]{1,0:T(8,128)(2,1)} %get-tuple-element.35.sg_ref, bf16[128,3200]{1,0:T(8,128)(2,1)} %get-tuple-element.33._.dg_ref, ...), custom_call_target="tpu_custom_call" | custom-call | flops 1000000000 | bytes 8000000 | tf_op jit(solution)/shard_map/inputs/pallas_call | solution.py:549
  145.7 4.4 %all-to-all-done.5.x_ref = bf16[128,8,128]{2,1,0:T(8,128)(2,1)S(1)} async-done(((bf16[128,8,128]{2,1,0:T(8,128)(2,1)}), bf16[128,8,128]{2,1,0:T(8,128)(2,1)S(1)}, u32[]{:S(2)}, u32[]{:S(2)}) %all-to-all-start.5) | async-done | bytes 262176 | tf_op jit(solution)/shard_map/all_to_all | solution.py:563
  150.1 0.9 unpack.1
Async XLA Ops:
  7.0 30.8 %all-to-all-start = ((bf16[32,8,3200]{2,1,0:T(8,128)(2,1)}), bf16[32,8,3200]{2,1,0:T(8,128)(2,1)S(1)}, u32[]{:S(2)}, u32[]{:S(2)}) async-start(bf16[32,8,3200]{2,1,0:T(8,128)(2,1)} %factors.1), calls=%async_computation | async-start | bytes 3276800 | tf_op jit(solution)/shard_map/all_to_all | solution.py:496
  37.8 21.8 %copy-start = (bf16[128,3200]{1,0:T(8,128)(2,1)S(1)}, bf16[128,3200]{1,0:T(8,128)(2,1)}, u32[]{:S(2)}) copy-start(bf16[128,3200]{1,0:T(8,128)(2,1)} %get-tuple-element.27._.do_ref) | copy-start | bytes 2457604
  37.8 21.8 %copy-start.5 = (bf16[128,128]{1,0:T(8,128)(2,1)S(1)}, bf16[128,128]{1,0:T(8,128)(2,1)}, u32[]{:S(2)}) copy-start(bf16[128,128]{1,0:T(8,128)(2,1)} %ow_ref.3) | copy-start | bytes 98308
  37.8 21.8 %copy-start.12 = (f32[128]{0:T(128)S(1)}, f32[128]{0:T(128)}, u32[]{:S(2)}) copy-start(f32[128]{0:T(128)} %param.17) | copy-start | bytes 1540
  61.9 18.9 %all-to-all-start.2 = ((bf16[32,4,3200]{2,1,0:T(4,128)(2,1)}), bf16[32,4,3200]{2,1,0:T(4,128)(2,1)S(1)}, u32[]{:S(2)}, u32[]{:S(2)}) async-start(bf16[32,4,3200]{2,1,0:T(4,128)(2,1)} %middle.1), calls=%async_computation.2 | async-start | bytes 1638400 | tf_op jit(solution)/shard_map/all_to_all | solution.py:522
  80.8 32.2 %copy-start.3 = (bf16[144,3200]{1,0:T(8,128)(2,1)S(1)}, bf16[144,3200]{1,0:T(8,128)(2,1)}, u32[]{:S(2)}) copy-start(bf16[144,3200]{1,0:T(8,128)(2,1)} %get-tuple-element.31.n_ref) | copy-start | bytes 2764804
  80.8 32.2 %copy-start.4 = (bf16[128,512]{1,0:T(8,128)(2,1)S(1)}, bf16[128,512]{1,0:T(8,128)(2,1)}, u32[]{:S(2)}) copy-start(bf16[128,512]{1,0:T(8,128)(2,1)} %w_ref.7) | copy-start | bytes 393220
  80.8 32.2 %copy-start.6 = (bf16[128,128]{1,0:T(8,128)(2,1)S(1)}, bf16[128,128]{1,0:T(8,128)(2,1)}, u32[]{:S(2)}) copy-start(bf16[128,128]{1,0:T(8,128)(2,1)} %gw_ref.5) | copy-start | bytes 98308
  80.8 32.2 %copy-start.7 = (f32[2,128,128]{2,1,0:T(8,128)S(1)}, f32[2,128,128]{2,1,0:T(8,128)}, u32[]{:S(2)}) copy-start(f32[2,128,128]{2,1,0:T(8,128)} %get-tuple-element.37.gv_ref) | copy-start | bytes 393220
  80.8 32.2 %copy-start.8 = (f32[144,128]{1,0:T(8,128)S(1)}, f32[144,128]{1,0:T(8,128)}, u32[]{:S(2)}) copy-start(f32[144,128]{1,0:T(8,128)} %get-tuple-element.38.gg_ref) | copy-start | bytes 221188
  80.8 32.2 %copy-start.9 = (f32[128,128]{1,0:T(8,128)S(1)}, f32[128,128]{1,0:T(8,128)}, u32[]{:S(2)}) copy-start(f32[128,128]{1,0:T(8,128)} %get-tuple-element.36.gow_ref) | copy-start | bytes 196612
  85.1 28.0 %copy-start.1 = (bf16[256,3200]{1,0:T(8,128)(2,1)S(1)}, bf16[256,3200]{1,0:T(8,128)(2,1)}, u32[]{:S(2)}) copy-start(bf16[256,3200]{1,0:T(8,128)(2,1)} %get-tuple-element.34.sv_ref) | copy-start | bytes 4915204
  85.1 28.0 %copy-start.2 = (bf16[256,3200]{1,0:T(8,128)(2,1)S(1)}, bf16[256,3200]{1,0:T(8,128)(2,1)}, u32[]{:S(2)}) copy-start(bf16[256,3200]{1,0:T(8,128)(2,1)} %get-tuple-element.35.sg_ref) | copy-start | bytes 4915204
  85.1 28.0 %copy-start.10 = (f32[128]{0:T(128)S(1)}, f32[128]{0:T(128)}, u32[]{:S(2)}) copy-start(f32[128]{0:T(128)} %param.13) | copy-start | bytes 1540
  85.1 28.0 %copy-start.11 = (f32[128]{0:T(128)S(1)}, f32[128]{0:T(128)}, u32[]{:S(2)}) copy-start(f32[128]{0:T(128)} %param.14) | copy-start | bytes 1540
  134.7 15.4 %all-to-all-start.5 = ((bf16[128,8,128]{2,1,0:T(8,128)(2,1)}), bf16[128,8,128]{2,1,0:T(8,128)(2,1)S(1)}, u32[]{:S(2)}, u32[]{:S(2)}) async-start(bf16[128,8,128]{2,1,0:T(8,128)(2,1)} %total.1), calls=%async_computation.5 | async-start | bytes 524288 | tf_op jit(solution)/shard_map/all_to_all | solution.py:563
